TPU v7x, 512 devices: a whole 4x8x8 slice. The times are simulated.
512 devices in a mesh: dp: 8 (over z_hi, core), mp: 64 (over z_lo, x, y).
Axes of the slice: x: 4, y: 8, z: 8 (z_hi: 4, z_lo: 2; z = z_hi * 2 + z_lo), core: 2. Of those that a mesh axis runs over, the one named last changes fastest.
Arguments:
- inputs: bfloat16 [2048, 4096], P('dp'), may hold values from -6 to 6
- upstream: bfloat16 [2048, 4096], P('dp'), may hold values from -6 to 6
- eig_tiles: bfloat16 [64, 8, 2, 128, 128], P('mp'), may hold values from -0.09375 to 0.09375
- eigvals: float32 [4096], replicated, may hold values from 0.25 to 4
Outputs:
- grad_t: bfloat16 [4096, 2048], P('mp', 'dp')
All inputs are finite; a program needn't handle non-finite values.
Results may differ from a plain program's by a relative error of at most 0.013.
Values may be sent and summed in bfloat16 or wider, within the bound.
No kernel may reach another device: no remote copies, remote signals or barrier semaphores. Data moves between devices by JAX's collectives and lax.ppermute only.
A program may use at most 64 MiB of HBM per device.

v0:
```python
import jax
import jax.numpy as jnp
from jax import lax
from jax.experimental import pallas as pl
from jax.experimental.pallas import tpu as pltpu
from jax.sharding import Mesh
from jax.sharding import PartitionSpec as P

F32 = jnp.float32
BF16 = jnp.bfloat16
AXES = ("zh", "core", "zl", "xh", "xl", "y")
SIZES = (4, 2, 2, 2, 2, 8)
ROWS = ("zl", "xh")
COLS = ("xl", "zl", "xh")
SWAP = [(0, 1), (1, 0)]

ANYWHERE = pl.BlockSpec(memory_space=pl.ANY)
IN_VMEM = pl.BlockSpec(memory_space=pltpu.VMEM)


def call(kernel, arrays, outs, scratch=()):
    held = [pltpu.with_memory_space_constraint(a, pltpu.VMEM) for a in arrays]
    single = not isinstance(outs, (list, tuple))
    shapes = [outs] if single else outs
    got = pl.pallas_call(
        kernel,
        out_shape=[pltpu.VMEM(s, d) for s, d in shapes_of(shapes)],
        in_specs=[IN_VMEM] * len(held),
        out_specs=[IN_VMEM] * len(shapes),
        scratch_shapes=list(scratch),
    )(*held)
    return got[0] if single else got


def shapes_of(outs):
    return [(o.shape, o.dtype) for o in outs]


def out(dtype, *shape):
    return jax.ShapeDtypeStruct(shape, dtype)


def project_kernel(x_ref, y_ref, eig_ref, out_ref, xs, tiles, sems, tile_sem):
    steps = eig_ref.shape[0]
    grid_rows = x_ref.shape[1] // (steps * 128)
    r = lax.axis_index("zl") * 2 + lax.axis_index("xh")

    def copy(s, la):
        src = x_ref if s == 0 else y_ref
        start = pl.multiple_of((la * grid_rows + r) * 128, 128)
        return pltpu.make_async_copy(
            src.at[:, pl.ds(start, 128)], xs.at[s, :, pl.ds(la * 128, 128)], sems.at[s, la]
        )

    load = pltpu.make_async_copy(eig_ref, tiles, tile_sem)
    load.start()
    for s in range(2):
        for la in range(steps):
            copy(s, la).start()
    load.wait()
    basis = jnp.concatenate(
        [tiles[:, lb].reshape(steps * 128, 128) for lb in range(tiles.shape[1])], 1
    )
    for s in range(2):
        for la in range(steps):
            copy(s, la).wait()
        part = jnp.dot(xs[s], basis, preferred_element_type=F32)
        turned = part.T.astype(BF16)
        out_ref[:, s] = turned.reshape(out_ref.shape[0], *out_ref.shape[2:])


def project(inputs, upstream, eig):
    tokens = inputs.shape[0]
    steps = eig.shape[0]
    return pl.pallas_call(
        project_kernel,
        out_shape=pltpu.VMEM((4, 2, 64, tokens), BF16),
        in_specs=[ANYWHERE] * 3,
        out_specs=IN_VMEM,
        scratch_shapes=[
            pltpu.VMEM((2, tokens, steps * 128), BF16),
            pltpu.VMEM(eig.shape, BF16),
            pltpu.SemaphoreType.DMA((2, steps)),
            pltpu.SemaphoreType.DMA,
        ],
        name="project",
    )(inputs, upstream, eig)


def spread_kernel(parts_ref, own_ref, copies_ref):
    total = parts_ref[0].astype(F32)
    for k in range(1, parts_ref.shape[0]):
        total += parts_ref[k].astype(F32)
    own = total.astype(BF16)
    own_ref[...] = own
    for k in range(copies_ref.shape[0]):
        copies_ref[k] = own


def gram_kernel(which):
    def kernel(b_ref, a_ref, out_ref):
        half = lax.axis_index("core") ^ which
        n = a_ref.shape[0] * a_ref.shape[2]
        tokens = a_ref.shape[3]
        over = (((1,), (1,)), ((), ()))
        left = b_ref[pl.ds(half * 4, 4)]
        block = lax.dot_general(
            left[:, 0].reshape(256, tokens),
            a_ref[:, 1].reshape(n, tokens),
            over,
            preferred_element_type=F32,
        )
        block += lax.dot_general(
            left[:, 1].reshape(256, tokens),
            a_ref[:, 0].reshape(n, tokens),
            over,
            preferred_element_type=F32,
        )
        out_ref[...] = block.astype(BF16)

    return kernel


def add_kernel(a_ref, b_ref, out_ref):
    total = a_ref[...].astype(F32) + b_ref[...].astype(F32)
    out_ref[...] = total.astype(BF16).reshape(out_ref.shape)


def roots_kernel(*refs):
    for k in range(3):
        refs[3 + k][...] = jnp.sqrt(refs[k][...])


def weigh_kernel(parts_ref, rows_ref, cols_ref, out_ref):
    share = parts_ref[0].astype(F32)
    for k in range(1, parts_ref.shape[0]):
        share += parts_ref[k].astype(F32)
    s_b, s_a = rows_ref[...], cols_ref[...]
    kernel = -1.0 / (s_b * s_a * (s_b + s_a))
    part = (kernel * (0.5 * share)).astype(BF16)
    for k in range(out_ref.shape[0]):
        out_ref[k] = part


def mix_kernel(half_ref, a_ref, other_ref, out_ref):
    core = lax.axis_index("core")
    tokens = a_ref.shape[3]
    weights = half_ref[...].reshape(256, -1)
    for to, proj_in in ((core, a_ref[:, 0]), (core ^ 1, other_ref[...])):
        part = jnp.dot(weights, proj_in.reshape(-1, tokens), preferred_element_type=F32)
        part = part.astype(BF16)
        for r in range(4):
            for xl in range(2):
                row = r * 64 + xl * 32
                out_ref[to, xl, r] = part[row : row + 32]


def update_kernel(factor, parts_ref, left_ref, root_ref, out_ref):
    zl, xh, xl = lax.axis_index("zl"), lax.axis_index("xh"), lax.axis_index("xl")
    rows = pl.ds(pl.multiple_of(xl * 32, 32), 32)
    for half in range(2):
        mixed = parts_ref[half, 0].astype(F32)
        for k in range(1, 8):
            mixed += parts_ref[half, k].astype(F32)
        up = left_ref[half * 4 + zl * 2 + xh, 1, rows].astype(F32)
        update = (up / root_ref[pl.ds(half * 32, 32)] + factor * mixed).astype(BF16)
        for k in range(out_ref.shape[0]):
            out_ref[k, half] = update


def split_l_kernel(kept_ref, came_ref, keep_ref, send_ref):
    zl, xl = lax.axis_index("zl"), lax.axis_index("xl")
    for from_z, ref in ((zl, kept_ref), (zl ^ 1, came_ref)):
        for to_h in range(2):
            keep_ref[from_z, to_h] = ref[to_h * 2 + xl]
            send_ref[from_z, to_h] = ref[to_h * 2 + (xl ^ 1)]


def split_h_kernel(kept_ref, came_ref, keep_ref, send_ref):
    xh, xl = lax.axis_index("xh"), lax.axis_index("xl")
    for from_l, ref in ((xl, kept_ref), (xl ^ 1, came_ref)):
        for from_z in range(2):
            keep_ref[from_z, from_l] = ref[from_z, xh]
            send_ref[from_z, from_l] = ref[from_z, xh ^ 1]


def finish_kernel(kept_ref, came_ref, every_ref, out_ref, basis):
    xh = lax.axis_index("xh")
    tokens = every_ref.shape[3]
    for from_h, ref in ((xh, kept_ref), (xh ^ 1, came_ref)):
        for from_z in range(2):
            blocks = [ref[from_z, from_l, lb] for from_l in range(2) for lb in range(2)]
            basis[from_z * 2 + from_h] = jnp.concatenate(blocks, 1)
    rows = [
        every_ref[xl * 4 + r, half] for half in range(2) for r in range(4) for xl in range(2)
    ]
    part = jnp.dot(
        basis[...].reshape(512, 512), jnp.concatenate(rows, 0), preferred_element_type=F32
    )
    out_ref[...] = part.astype(BF16).reshape(-1, 64, tokens)


def on_device(inputs, upstream, eig_tiles, eigvals):
    zl, xh, xl, y = (lax.axis_index(a) for a in ("zl", "xh", "xl", "y"))
    zh, core = lax.axis_index("zh"), lax.axis_index("core")
    tokens = inputs.shape[0]
    eig = eig_tiles[0]
    r = zl * 2 + xh

    by_b = lax.dynamic_index_in_dim(eigvals.reshape(2, 2, 8, 128), y, 2, keepdims=False)
    lam_b = jnp.transpose(by_b, (1, 0, 2)).reshape(8, 64)
    cube = jnp.transpose(eigvals.reshape(2, 2, 8, 2, 64), (0, 3, 1, 2, 4)).reshape(8, 8, 64)
    lam_a = lax.dynamic_index_in_dim(cube, r * 2 + xl, 0, keepdims=False)
    by_half = lax.dynamic_index_in_dim(lam_b.reshape(2, 4, 2, 32), r, 1, keepdims=False)
    lam_own = lax.dynamic_index_in_dim(by_half, xl, 1, keepdims=False).reshape(64, 1)
    lam_rows = lax.dynamic_index_in_dim(lam_b, core * 4 + zh, 0, keepdims=False).reshape(64, 1)
    lam_cols = lam_a.reshape(1, 512)

    parts = project(inputs, upstream, eig)
    got = lax.all_to_all(parts, ROWS, 0, 0, tiled=True)
    own, copies = call(
        spread_kernel, (got,), (out(BF16, 2, 64, tokens), out(BF16, 8, 2, 64, tokens))
    )
    halves = eig.reshape(2, 4, 2, 128, 128)
    right = lax.all_to_all(copies, "y", 0, 0, tiled=True)
    away = lax.dynamic_index_in_dim(halves, 1 - zl, 0, keepdims=False)
    kept = lax.dynamic_index_in_dim(halves, zl, 0, keepdims=False)
    came = lax.ppermute(away, "zl", SWAP)
    quarter = out(BF16, 2, 2, 2, 128, 128)
    keep_l, send_l = call(split_l_kernel, (kept, came), (quarter, quarter))
    got_l = lax.ppermute(send_l, "xl", SWAP)
    s_rows, s_cols, s_own = call(
        roots_kernel,
        (lam_rows, lam_cols, lam_own),
        (out(F32, 64, 1), out(F32, 1, 512), out(F32, 64, 1)),
    )
    again = jnp.broadcast_to(own[None], (8, *own.shape))
    left = lax.all_to_all(again, COLS, 0, 0, tiled=True)

    half_block = out(BF16, 256, 512)
    send = call(gram_kernel(1), (left, right), half_block)
    other = lax.ppermute(send, "core", SWAP)
    keep = call(gram_kernel(0), (left, right), half_block)
    both = call(add_kernel, (keep, other), out(BF16, 4, 64, 512))

    shares = lax.all_to_all(both, "zh", 0, 0, tiled=True)
    keep_h, send_h = call(split_h_kernel, (keep_l, got_l), (quarter, quarter))
    got_h = lax.ppermute(send_h, "xh", SWAP)
    other_in = lax.ppermute(right[:, 0], "core", SWAP)
    part = call(weigh_kernel, (shares, s_rows, s_cols), out(BF16, 4, 64, 512))
    mine = lax.all_to_all(part, "zh", 0, 0, tiled=True)
    mixed_part = call(mix_kernel, (mine, right, other_in), out(BF16, 2, 2, 4, 32, tokens))
    mixed = lax.all_to_all(mixed_part.reshape(16, 32, tokens), ("core", *COLS), 0, 0, tiled=True)
    factor = 2.0 / (8 * tokens)
    update = call(
        lambda *refs: update_kernel(factor, *refs),
        (mixed.reshape(2, 8, 32, tokens), left, s_own),
        out(BF16, 8, 2, 32, tokens),
    )
    every = lax.all_to_all(update, COLS, 0, 0, tiled=True)
    grad_part = call(
        finish_kernel,
        (keep_h, got_h, every),
        out(BF16, 8, 64, tokens),
        (pltpu.VMEM((4, 128, 512), BF16),),
    )
    blocks = lax.all_to_all(grad_part, "y", 0, 0, tiled=True)
    return jnp.sum(blocks.astype(F32), 0).astype(BF16)


def solution(mesh):
    grid = Mesh(mesh.devices.reshape(SIZES), AXES)
    dp, mp = AXES[:2], AXES[2:]
    return jax.shard_map(
        on_device,
        mesh=grid,
        in_specs=(P(dp, None), P(dp, None), P(mp, None, None, None, None), P()),
        out_specs=P(mp, dp),
        check_vma=False,
    )
```

profile of v0, /device:TPU:64, one launch (start us, length us, event | category | flops | bytes accessed | tf_op | source)
XLA Modules:
  0.0 140.2 jit_solution(17149554474568282110)
XLA Ops:
  0.0 2.7 %project.1 = bf16[4,2,64,256]{3,2,1,0:T(8,128)(2,1)S(1)} custom-call(bf16[256,4096]{1,0:T(8,128)(2,1)} %x_ref.1, bf16[256,4096]{1,0:T(8,128)(2,1)} %y_ref.1, bf16[8,2,128,128]{3,2,1,0:T(8,128)(2,1)} %bitcast.21), custom_call_target="tpu_custom_call" | custom-call | tf_op jit(solution)/shard_map/project/pallas_call | solution.py:75
  2.7 13.5 %all_to_all.40.parts_ref = bf16[4,2,64,256]{3,2,1,0:T(8,128)(2,1)S(1)} all-to-all(bf16[4,2,64,256]{3,2,1,0:T(8,128)(2,1)S(1)} %project.1), channel_id=1, replica_groups=mesh['zh'=4,'core'=2,'zl'=2,'xh'=2,'xl'=2,'y'=8] {'zl','xh'}, dimensions={0} | all-to-all | bytes 524288 | tf_op jit(solution)/shard_map/all_to_all | solution.py:220
  16.2 21.4 %all_to_all.41.a_ref = bf16[8,2,64,256]{3,2,1,0:T(8,128)(2,1)S(1)} all-to-all(bf16[8,2,64,256]{3,2,1,0:T(8,128)(2,1)S(1)} %get-tuple-element.19), channel_id=1, replica_groups=mesh['zh'=4,'core'=2,'zl'=2,'xh'=2,'xl'=2,'y'=8] {'y'}, dimensions={0} | all-to-all | bytes 1048576 | tf_op jit(solution)/shard_map/all_to_all | solution.py:225
  37.7 10.8 %all_to_all.42.b_ref.refs_1_ = bf16[8,2,64,256]{3,2,1,0:T(8,128)(2,1)S(1)} all-to-all(bf16[8,2,64,256]{3,2,1,0:T(8,128)(2,1)S(1)} %broadcast_in_dim.2), channel_id=1, replica_groups=mesh['zh'=4,'core'=2,'zl'=2,'xh'=2,'xl'=2,'y'=8] {'xl','zl','xh'}, dimensions={0} | all-to-all | bytes 1048576 | tf_op jit(solution)/shard_map/all_to_all | solution.py:238
  48.9 1.9 %collective-permute-start.3 = (bf16[256,512]{1,0:T(8,128)(2,1)S(1)}, bf16[256,512]{1,0:T(8,128)(2,1)S(1)}, u32[]{:S(2)}, u32[]{:S(2)}) collective-permute-start(bf16[256,512]{1,0:T(8,128)(2,1)S(1)} %shard_map.50), channel_id=1, source_target_pairs={{0,64},{64,0},{1,65},{65,1},{2,66},{66,2},{3,67},{67,3},{4,68},{68... | collective-permute-start | bytes 786440 | tf_op jit(solution)/shard_map/ppermute | solution.py:242
  51.1 1.2 collective-permute-done.3.b_ref
  52.3 0.8 shard_map.51
  53.1 9.5 %all-to-all-start.3 = ((bf16[4,64,512]{2,1,0:T(8,128)(2,1)}), bf16[4,64,512]{2,1,0:T(8,128)(2,1)S(1)}, u32[]{:S(2)}, u32[]{:S(2)}) async-start(bf16[4,64,512]{2,1,0:T(8,128)(2,1)} %shard_map.51), calls=%async_computation.3 | async-start | bytes 524288 | tf_op jit(solution)/shard_map/all_to_all | solution.py:246
  63.3 10.1 %all-to-all-done.3.parts_ref = bf16[4,64,512]{2,1,0:T(8,128)(2,1)S(1)} async-done(((bf16[4,64,512]{2,1,0:T(8,128)(2,1)}), bf16[4,64,512]{2,1,0:T(8,128)(2,1)S(1)}, u32[]{:S(2)}, u32[]{:S(2)}) %all-to-all-start.3) | async-done | bytes 262176 | tf_op jit(solution)/shard_map/all_to_all | solution.py:246
  73.4 0.8 shard_map.53
  74.2 3.4 %all-to-all-start.4 = ((bf16[4,64,512]{2,1,0:T(8,128)(2,1)}), bf16[4,64,512]{2,1,0:T(8,128)(2,1)S(1)}, u32[]{:S(2)}, u32[]{:S(2)}) async-start(bf16[4,64,512]{2,1,0:T(8,128)(2,1)} %shard_map.53), calls=%async_computation.4 | async-start | bytes 524288 | tf_op jit(solution)/shard_map/all_to_all | solution.py:251
  77.7 1.9 %collective-permute-start.4 = (bf16[8,64,256]{2,1,0:T(8,128)(2,1)S(1)}, bf16[8,64,256]{2,1,0:T(8,128)(2,1)S(1)}, u32[]{:S(2)}, u32[]{:S(2)}) collective-permute-start(bf16[8,64,256]{2,1,0:T(8,128)(2,1)S(1)} %slice_bitcast_fusion), channel_id=1, source_target_pairs={{0,64},{64,0},{1,65},{65,1},{2,66},{66,2},{3,67},{67,3},{4,68},{68... | collective-permute-start | bytes 786440 | tf_op jit(solution)/shard_map/ppermute | solution.py:249
  79.6 1.5 %collective-permute-done.4.other_ref = bf16[8,64,256]{2,1,0:T(8,128)(2,1)S(1)} collective-permute-done((bf16[8,64,256]{2,1,0:T(8,128)(2,1)S(1)}, bf16[8,64,256]{2,1,0:T(8,128)(2,1)S(1)}, u32[]{:S(2)}, u32[]{:S(2)}) %collective-permute-start.4) | collective-permute-done | bytes 262176 | tf_op jit(solution)/shard_map/ppermute | solution.py:249
  81.1 6.7 %all-to-all-done.4.half_ref = bf16[4,64,512]{2,1,0:T(8,128)(2,1)S(1)} async-done(((bf16[4,64,512]{2,1,0:T(8,128)(2,1)}), bf16[4,64,512]{2,1,0:T(8,128)(2,1)S(1)}, u32[]{:S(2)}, u32[]{:S(2)}) %all-to-all-start.4) | async-done | bytes 262176 | tf_op jit(solution)/shard_map/all_to_all | solution.py:251
  87.8 1.0 shard_map.54
  88.9 4.7 %all-to-all-start.5 = ((bf16[16,32,256]{2,1,0:T(8,128)(2,1)}), bf16[16,32,256]{2,1,0:T(8,128)(2,1)S(1)}, u32[]{:S(2)}, u32[]{:S(2)}) async-start(bf16[16,32,256]{2,1,0:T(8,128)(2,1)} %bitcast.11), calls=%async_computation.5 | async-start | bytes 524288 | tf_op jit(solution)/shard_map/all_to_all | solution.py:253
  93.6 2.1 %collective-permute-start = (bf16[4,2,128,128]{3,2,1,0:T(8,128)(2,1)S(1)}, bf16[4,2,128,128]{3,2,1,0:T(8,128)(2,1)S(1)}, u32[]{:S(2)}, u32[]{:S(2)}) collective-permute-start(bf16[4,2,128,128]{3,2,1,0:T(8,128)(2,1)S(1)} %get-tuple-element.23), channel_id=1, source_target_pairs={{0,32},{32,0},{1,33},{33,1},{2,34},{34,2},{3,35},{35,3},{4,36},{36... | collective-permute-start | bytes 786440 | tf_op jit(solution)/shard_map/ppermute | solution.py:228
  95.8 8.1 %collective-permute-done.came_ref = bf16[4,2,128,128]{3,2,1,0:T(8,128)(2,1)S(1)} collective-permute-done((bf16[4,2,128,128]{3,2,1,0:T(8,128)(2,1)S(1)}, bf16[4,2,128,128]{3,2,1,0:T(8,128)(2,1)S(1)}, u32[]{:S(2)}, u32[]{:S(2)}) %collective-permute-start) | collective-permute-done | bytes 262176 | tf_op jit(solution)/shard_map/ppermute | solution.py:228
  103.9 3.4 %collective-permute-start.1 = (bf16[2,2,2,128,128]{4,3,2,1,0:T(8,128)(2,1)S(1)}, bf16[2,2,2,128,128]{4,3,2,1,0:T(8,128)(2,1)S(1)}, u32[]{:S(2)}, u32[]{:S(2)}) collective-permute-start(bf16[2,2,2,128,128]{4,3,2,1,0:T(8,128)(2,1)S(1)} %get-tuple-element.15), channel_id=1, source_target_pairs={{0,8},{8,0},{1,9},{9,1},{2,10},{10,2},{3,11},{11,3},{4,12},{12,4},... | collective-permute-start | bytes 786440 | tf_op jit(solution)/shard_map/ppermute | solution.py:231
  107.4 0.8 shard_map.55
  108.2 5.4 %all-to-all-start.6 = ((bf16[8,2,32,256]{3,2,1,0:T(8,128)(2,1)}), bf16[8,2,32,256]{3,2,1,0:T(8,128)(2,1)S(1)}, u32[]{:S(2)}, u32[]{:S(2)}) async-start(bf16[8,2,32,256]{3,2,1,0:T(8,128)(2,1)} %shard_map.55), calls=%async_computation.6 | async-start | bytes 524288 | tf_op jit(solution)/shard_map/all_to_all | solution.py:260
  113.6 4.9 %collective-permute-start.2 = (bf16[2,2,2,128,128]{4,3,2,1,0:T(8,128)(2,1)S(1)}, bf16[2,2,2,128,128]{4,3,2,1,0:T(8,128)(2,1)S(1)}, u32[]{:S(2)}, u32[]{:S(2)}) collective-permute-start(bf16[2,2,2,128,128]{4,3,2,1,0:T(8,128)(2,1)S(1)} %get-tuple-element.17), channel_id=1, source_target_pairs={{0,16},{16,0},{1,17},{17,1},{2,18},{18,2},{3,19},{19,3},{4,20},{20... | collective-permute-start | bytes 786440 | tf_op jit(solution)/shard_map/ppermute | solution.py:248
  118.5 6.8 %collective-permute-done.2.came_ref = bf16[2,2,2,128,128]{4,3,2,1,0:T(8,128)(2,1)S(1)} collective-permute-done((bf16[2,2,2,128,128]{4,3,2,1,0:T(8,128)(2,1)S(1)}, bf16[2,2,2,128,128]{4,3,2,1,0:T(8,128)(2,1)S(1)}, u32[]{:S(2)}, u32[]{:S(2)}) %collective-permute-start.2) | collective-permute-done | bytes 262176 | tf_op jit(solution)/shard_map/ppermute | solution.py:248
  125.6 13.9 %all_to_all.43 = bf16[8,64,256]{2,1,0:T(8,128)(2,1)S(1)} all-to-all(bf16[8,64,256]{2,1,0:T(8,128)(2,1)S(1)} %shard_map.56), channel_id=1, replica_groups=mesh['zh'=4,'core'=2,'zl'=2,'xh'=2,'xl'=2,'y'=8] {'y'}, dimensions={0} | all-to-all | bytes 524288 | tf_op jit(solution)/shard_map/all_to_all | solution.py:267
  (30 shorter events, 2.5 us)
Async XLA Ops:
  48.5 14.1 %copy-start.1 = (f32[4096]{0:T(1024)S(1)}, f32[4096]{0:T(1024)}, u32[]{:S(2)}) copy-start(f32[4096]{0:T(1024)} %param.7) | copy-start | bytes 49156
  48.9 3.4 %collective-permute-start.3 = (bf16[256,512]{1,0:T(8,128)(2,1)S(1)}, bf16[256,512]{1,0:T(8,128)(2,1)S(1)}, u32[]{:S(2)}, u32[]{:S(2)}) collective-permute-start(bf16[256,512]{1,0:T(8,128)(2,1)S(1)} %shard_map.50), channel_id=1, source_target_pairs={{0,64},{64,0},{1,65},{65,1},{2,66},{66,2},{3,67},{67,3},{4,68},{68... | collective-permute-start | bytes 786440 | tf_op jit(solution)/shard_map/ppermute | solution.py:242
  53.1 40.5 %copy-start = (bf16[1,8,2,128,128]{4,3,2,1,0:T(8,128)(2,1)S(1)}, bf16[1,8,2,128,128]{4,3,2,1,0:T(8,128)(2,1)}, u32[]{:S(2)}) copy-start(bf16[1,8,2,128,128]{4,3,2,1,0:T(8,128)(2,1)} %param.6) | copy-start | bytes 1572868
  53.1 20.3 %all-to-all-start.3 = ((bf16[4,64,512]{2,1,0:T(8,128)(2,1)}), bf16[4,64,512]{2,1,0:T(8,128)(2,1)S(1)}, u32[]{:S(2)}, u32[]{:S(2)}) async-start(bf16[4,64,512]{2,1,0:T(8,128)(2,1)} %shard_map.51), calls=%async_computation.3 | async-start | bytes 524288 | tf_op jit(solution)/shard_map/all_to_all | solution.py:246
  74.2 13.6 %all-to-all-start.4 = ((bf16[4,64,512]{2,1,0:T(8,128)(2,1)}), bf16[4,64,512]{2,1,0:T(8,128)(2,1)S(1)}, u32[]{:S(2)}, u32[]{:S(2)}) async-start(bf16[4,64,512]{2,1,0:T(8,128)(2,1)} %shard_map.53), calls=%async_computation.4 | async-start | bytes 524288 | tf_op jit(solution)/shard_map/all_to_all | solution.py:251
  77.7 3.4 %collective-permute-start.4 = (bf16[8,64,256]{2,1,0:T(8,128)(2,1)S(1)}, bf16[8,64,256]{2,1,0:T(8,128)(2,1)S(1)}, u32[]{:S(2)}, u32[]{:S(2)}) collective-permute-start(bf16[8,64,256]{2,1,0:T(8,128)(2,1)S(1)} %slice_bitcast_fusion), channel_id=1, source_target_pairs={{0,64},{64,0},{1,65},{65,1},{2,66},{66,2},{3,67},{67,3},{4,68},{68... | collective-permute-start | bytes 786440 | tf_op jit(solution)/shard_map/ppermute | solution.py:249
  88.9 18.5 %all-to-all-start.5 = ((bf16[16,32,256]{2,1,0:T(8,128)(2,1)}), bf16[16,32,256]{2,1,0:T(8,128)(2,1)S(1)}, u32[]{:S(2)}, u32[]{:S(2)}) async-start(bf16[16,32,256]{2,1,0:T(8,128)(2,1)} %bitcast.11), calls=%async_computation.5 | async-start | bytes 524288 | tf_op jit(solution)/shard_map/all_to_all | solution.py:253
  93.6 10.3 %collective-permute-start = (bf16[4,2,128,128]{3,2,1,0:T(8,128)(2,1)S(1)}, bf16[4,2,128,128]{3,2,1,0:T(8,128)(2,1)S(1)}, u32[]{:S(2)}, u32[]{:S(2)}) collective-permute-start(bf16[4,2,128,128]{3,2,1,0:T(8,128)(2,1)S(1)} %get-tuple-element.23), channel_id=1, source_target_pairs={{0,32},{32,0},{1,33},{33,1},{2,34},{34,2},{3,35},{35,3},{4,36},{36... | collective-permute-start | bytes 786440 | tf_op jit(solution)/shard_map/ppermute | solution.py:228
  103.9 9.6 %collective-permute-start.1 = (bf16[2,2,2,128,128]{4,3,2,1,0:T(8,128)(2,1)S(1)}, bf16[2,2,2,128,128]{4,3,2,1,0:T(8,128)(2,1)S(1)}, u32[]{:S(2)}, u32[]{:S(2)}) collective-permute-start(bf16[2,2,2,128,128]{4,3,2,1,0:T(8,128)(2,1)S(1)} %get-tuple-element.15), channel_id=1, source_target_pairs={{0,8},{8,0},{1,9},{9,1},{2,10},{10,2},{3,11},{11,3},{4,12},{12,4},... | collective-permute-start | bytes 786440 | tf_op jit(solution)/shard_map/ppermute | solution.py:231
  108.2 17.1 %all-to-all-start.6 = ((bf16[8,2,32,256]{3,2,1,0:T(8,128)(2,1)}), bf16[8,2,32,256]{3,2,1,0:T(8,128)(2,1)S(1)}, u32[]{:S(2)}, u32[]{:S(2)}) async-start(bf16[8,2,32,256]{3,2,1,0:T(8,128)(2,1)} %shard_map.55), calls=%async_computation.6 | async-start | bytes 524288 | tf_op jit(solution)/shard_map/all_to_all | solution.py:260
  113.6 11.6 %collective-permute-start.2 = (bf16[2,2,2,128,128]{4,3,2,1,0:T(8,128)(2,1)S(1)}, bf16[2,2,2,128,128]{4,3,2,1,0:T(8,128)(2,1)S(1)}, u32[]{:S(2)}, u32[]{:S(2)}) collective-permute-start(bf16[2,2,2,128,128]{4,3,2,1,0:T(8,128)(2,1)S(1)} %get-tuple-element.17), channel_id=1, source_target_pairs={{0,16},{16,0},{1,17},{17,1},{2,18},{18,2},{3,19},{19,3},{4,20},{20... | collective-permute-start | bytes 786440 | tf_op jit(solution)/shard_map/ppermute | solution.py:248
where the time goes:
time: 141 us; the launch traced here: 140 us
  blocking collectives  59.7 us (42%)
  starting transfers between devices  37.3 us (26%)
  waiting for transfers between devices  34.4 us (24%)
  Pallas kernels  7.2 us (5%)
    all_to_all x1, blocking collectives, on_device(): right = lax.all_to_all(copies, 'y', 0, 0, tiled=True)  21.4 us
    all_to_all x1, blocking collectives, on_device(): blocks = lax.all_to_all(grad_part, 'y', 0, 0, tiled=True)  13.9 us
    all_to_all x1, blocking collectives, on_device(): got = lax.all_to_all(parts, ROWS, 0, 0, tiled=True)  13.5 us
    all_to_all x1, blocking collectives, on_device(): left = lax.all_to_all(again, COLS, 0, 0, tiled=True)  10.8 us
    all_to_all x1, waiting for transfers between devices, on_device(): shares = lax.all_to_all(both, 'zh', 0, 0, tiled=True)  10.1 us
    all_to_all x1, starting transfers between devices, on_device(): shares = lax.all_to_all(both, 'zh', 0, 0, tiled=True)  9.53 us
    ppermute x1, waiting for transfers between devices, on_device(): came = lax.ppermute(away, 'zl', SWAP)  8.14 us
    ppermute x1, waiting for transfers between devices, on_device(): got_h = lax.ppermute(send_h, 'xh', SWAP)  6.76 us
  transfers between devices with their start and end apart: 9, of which 6 were waited for; matrix products, arithmetic and copies ran while one was open for 0% of the time, Pallas kernels for 1%

commit v1 on v0

--- a/solution.py
+++ b/solution.py
@@ -97,33 +97,25 @@
         copies_ref[k] = own
 
 
-def gram_kernel(which):
-    def kernel(b_ref, a_ref, out_ref):
-        half = lax.axis_index("core") ^ which
-        n = a_ref.shape[0] * a_ref.shape[2]
-        tokens = a_ref.shape[3]
-        over = (((1,), (1,)), ((), ()))
-        left = b_ref[pl.ds(half * 4, 4)]
-        block = lax.dot_general(
-            left[:, 0].reshape(256, tokens),
-            a_ref[:, 1].reshape(n, tokens),
-            over,
-            preferred_element_type=F32,
-        )
-        block += lax.dot_general(
-            left[:, 1].reshape(256, tokens),
-            a_ref[:, 0].reshape(n, tokens),
-            over,
-            preferred_element_type=F32,
-        )
-        out_ref[...] = block.astype(BF16)
-
-    return kernel
-
-
-def add_kernel(a_ref, b_ref, out_ref):
-    total = a_ref[...].astype(F32) + b_ref[...].astype(F32)
-    out_ref[...] = total.astype(BF16).reshape(out_ref.shape)
+def again_kernel(own_ref, out_ref):
+    for core in range(2):
+        for k in range(8):
+            out_ref[core * 8 + k] = own_ref[:, core * 32 : core * 32 + 32]
+
+
+def gram_kernel(b_ref, a_ref, other_ref, out_ref):
+    core = lax.axis_index("core")
+    tokens = a_ref.shape[3]
+    block = jnp.zeros(out_ref.shape, F32).reshape(256, -1)
+    for of, ref in ((core, a_ref), (core ^ 1, other_ref)):
+        for s in range(2):
+            block += lax.dot_general(
+                b_ref[of, :, s].reshape(256, tokens),
+                ref[:, 1 - s].reshape(-1, tokens),
+                (((1,), (1,)), ((), ())),
+                preferred_element_type=F32,
+            )
+    out_ref[...] = block.astype(BF16).reshape(out_ref.shape)
 
 
 def roots_kernel(*refs):
@@ -146,26 +138,22 @@
     core = lax.axis_index("core")
     tokens = a_ref.shape[3]
     weights = half_ref[...].reshape(256, -1)
-    for to, proj_in in ((core, a_ref[:, 0]), (core ^ 1, other_ref[...])):
-        part = jnp.dot(weights, proj_in.reshape(-1, tokens), preferred_element_type=F32)
-        part = part.astype(BF16)
-        for r in range(4):
-            for xl in range(2):
-                row = r * 64 + xl * 32
-                out_ref[to, xl, r] = part[row : row + 32]
-
-
-def update_kernel(factor, parts_ref, left_ref, root_ref, out_ref):
-    zl, xh, xl = lax.axis_index("zl"), lax.axis_index("xh"), lax.axis_index("xl")
-    rows = pl.ds(pl.multiple_of(xl * 32, 32), 32)
+    for to, ref in ((core, a_ref), (core ^ 1, other_ref)):
+        proj_in = ref[:, 0].reshape(-1, tokens)
+        part = jnp.dot(weights, proj_in, preferred_element_type=F32)
+        out_ref[to] = part.astype(BF16).reshape(8, 32, tokens)
+
+
+def update_kernel(factor, parts_ref, own_ref, root_ref, out_ref):
     for half in range(2):
         mixed = parts_ref[half, 0].astype(F32)
         for k in range(1, 8):
             mixed += parts_ref[half, k].astype(F32)
-        up = left_ref[half * 4 + zl * 2 + xh, 1, rows].astype(F32)
-        update = (up / root_ref[pl.ds(half * 32, 32)] + factor * mixed).astype(BF16)
+        rows = pl.ds(half * 32, 32)
+        update = own_ref[1, rows].astype(F32) / root_ref[rows] + factor * mixed
+        update = update.astype(BF16)
         for k in range(out_ref.shape[0]):
-            out_ref[k, half] = update
+            out_ref[k, rows] = update
 
 
 def split_l_kernel(kept_ref, came_ref, keep_ref, send_ref):
@@ -186,16 +174,15 @@
 
 def finish_kernel(kept_ref, came_ref, every_ref, out_ref, basis):
     xh = lax.axis_index("xh")
-    tokens = every_ref.shape[3]
+    tokens = every_ref.shape[2]
     for from_h, ref in ((xh, kept_ref), (xh ^ 1, came_ref)):
         for from_z in range(2):
             blocks = [ref[from_z, from_l, lb] for from_l in range(2) for lb in range(2)]
             basis[from_z * 2 + from_h] = jnp.concatenate(blocks, 1)
-    rows = [
-        every_ref[xl * 4 + r, half] for half in range(2) for r in range(4) for xl in range(2)
-    ]
     part = jnp.dot(
-        basis[...].reshape(512, 512), jnp.concatenate(rows, 0), preferred_element_type=F32
+        basis[...].reshape(512, 512),
+        every_ref[...].reshape(512, tokens),
+        preferred_element_type=F32,
     )
     out_ref[...] = part.astype(BF16).reshape(-1, 64, tokens)
 
@@ -211,9 +198,9 @@
     lam_b = jnp.transpose(by_b, (1, 0, 2)).reshape(8, 64)
     cube = jnp.transpose(eigvals.reshape(2, 2, 8, 2, 64), (0, 3, 1, 2, 4)).reshape(8, 8, 64)
     lam_a = lax.dynamic_index_in_dim(cube, r * 2 + xl, 0, keepdims=False)
-    by_half = lax.dynamic_index_in_dim(lam_b.reshape(2, 4, 2, 32), r, 1, keepdims=False)
-    lam_own = lax.dynamic_index_in_dim(by_half, xl, 1, keepdims=False).reshape(64, 1)
-    lam_rows = lax.dynamic_index_in_dim(lam_b, core * 4 + zh, 0, keepdims=False).reshape(64, 1)
+    lam_own = lax.dynamic_index_in_dim(lam_a, y, 0, keepdims=False).reshape(64, 1)
+    by_core = lax.dynamic_index_in_dim(lam_b.reshape(4, 2, 2, 32), core, 2, keepdims=False)
+    lam_rows = lax.dynamic_index_in_dim(by_core, zh, 0, keepdims=False).reshape(64, 1)
     lam_cols = lam_a.reshape(1, 512)
 
     parts = project(inputs, upstream, eig)
@@ -234,28 +221,25 @@
         (lam_rows, lam_cols, lam_own),
         (out(F32, 64, 1), out(F32, 1, 512), out(F32, 64, 1)),
     )
-    again = jnp.broadcast_to(own[None], (8, *own.shape))
-    left = lax.all_to_all(again, COLS, 0, 0, tiled=True)
-
-    half_block = out(BF16, 256, 512)
-    send = call(gram_kernel(1), (left, right), half_block)
-    other = lax.ppermute(send, "core", SWAP)
-    keep = call(gram_kernel(0), (left, right), half_block)
-    both = call(add_kernel, (keep, other), out(BF16, 4, 64, 512))
+    again = call(again_kernel, (own,), out(BF16, 16, 2, 32, tokens))
+    left = lax.all_to_all(again, ("core", *COLS), 0, 0, tiled=True)
+    other = lax.ppermute(right, "core", SWAP)
+    both = call(
+        gram_kernel, (left.reshape(2, 8, 2, 32, tokens), right, other), out(BF16, 4, 64, 512)
+    )
 
     shares = lax.all_to_all(both, "zh", 0, 0, tiled=True)
     keep_h, send_h = call(split_h_kernel, (keep_l, got_l), (quarter, quarter))
     got_h = lax.ppermute(send_h, "xh", SWAP)
-    other_in = lax.ppermute(right[:, 0], "core", SWAP)
     part = call(weigh_kernel, (shares, s_rows, s_cols), out(BF16, 4, 64, 512))
     mine = lax.all_to_all(part, "zh", 0, 0, tiled=True)
-    mixed_part = call(mix_kernel, (mine, right, other_in), out(BF16, 2, 2, 4, 32, tokens))
+    mixed_part = call(mix_kernel, (mine, right, other), out(BF16, 2, 8, 32, tokens))
     mixed = lax.all_to_all(mixed_part.reshape(16, 32, tokens), ("core", *COLS), 0, 0, tiled=True)
     factor = 2.0 / (8 * tokens)
     update = call(
         lambda *refs: update_kernel(factor, *refs),
-        (mixed.reshape(2, 8, 32, tokens), left, s_own),
-        out(BF16, 8, 2, 32, tokens),
+        (mixed.reshape(2, 8, 32, tokens), own, s_own),
+        out(BF16, 8, 64, tokens),
     )
     every = lax.all_to_all(update, COLS, 0, 0, tiled=True)
     grad_part = call(

time: 141 us -> 140 us (level)
  blocking collectives: 59.7 us -> 39.4 us
  waiting for transfers between devices: 34.4 us -> 49.1 us
  starting transfers between devices: 37.3 us -> 41.6 us
    all_to_all x2 -> x1, blocking collectives: 32.3 us -> 12.1 us  [on_device(): mine = lax.all_to_all(part, 'zh', 0, 0, tiled=True)]
    all_to_all x1 -> x2, waiting for transfers between devices: 6.74 us -> 23.9 us  [the longest x1 15.5 us: on_device(): right = lax.all_to_all(copies, 'y', 0, 0, tiled=True)]
    all_to_all x1 -> x2, starting transfers between devices: 3.42 us -> 9.56 us  [the longest x1 5.27 us: on_device(): right = lax.all_to_all(copies, 'y', 0, 0, tiled=True)]
    ppermute x2 -> x1, waiting for transfers between devices: 2.66 us -> 0.01 us  [on_device(): other = lax.ppermute(right, 'core', SWAP)]
    ppermute x2 -> x1, starting transfers between devices: 3.84 us -> 2.07 us  [on_device(): other = lax.ppermute(right, 'core', SWAP)]
    pallas_call x11 -> x10, Pallas kernels: 4.54 us -> 5.19 us  [call(): pl.pallas_call(kernel, out_shape=[pltpu.VMEM(s, d) for s, d in shapes_of(...]
  transfers between devices with their start and end apart: 9 -> 9, of which waited for: 6 -> 5; matrix products, arithmetic and copies ran while one was open for 0% -> 0% of each run, Pallas kernels for 1% -> 1%
where the time goes in v1:
time: 140 us; the launch traced here: 139 us
  waiting for transfers between devices  49.1 us (35%)
  starting transfers between devices  41.6 us (30%)
  blocking collectives  39.4 us (28%)
  Pallas kernels  7.85 us (6%)
    all_to_all x1, waiting for transfers between devices, on_device(): right = lax.all_to_all(copies, 'y', 0, 0, tiled=True)  15.5 us
    all_to_all x1, blocking collectives, on_device(): blocks = lax.all_to_all(grad_part, 'y', 0, 0, tiled=True)  13.9 us
    all_to_all x1, blocking collectives, on_device(): got = lax.all_to_all(parts, ROWS, 0, 0, tiled=True)  13.5 us
    all_to_all x1, blocking collectives, on_device(): mine = lax.all_to_all(part, 'zh', 0, 0, tiled=True)  12.1 us
    all_to_all x1, waiting for transfers between devices, on_device(): shares = lax.all_to_all(both, 'zh', 0, 0, tiled=True)  10.2 us
    all_to_all x1, starting transfers between devices, on_device(): shares = lax.all_to_all(both, 'zh', 0, 0, tiled=True)  9.54 us
    all_to_all x1, waiting for transfers between devices, on_device(): left = lax.all_to_all(again, ('core', *COLS), 0, 0, tiled=True)  8.43 us
    ppermute x1, waiting for transfers between devices, on_device(): came = lax.ppermute(away, 'zl', SWAP)  8.14 us
  transfers between devices with their start and end apart: 9, of which 5 were waited for; matrix products, arithmetic and copies ran while one was open for 0% of the time, Pallas kernels for 1%

profile of v1, /device:TPU:64, one launch (start us, length us, event | category | flops | bytes accessed | tf_op | source)
XLA Modules:
  0.0 139.3 jit_solution(15703125473786656209)
XLA Ops:
  0.0 2.7 %project.1 = bf16[4,2,64,256]{3,2,1,0:T(8,128)(2,1)S(1)} custom-call(bf16[256,4096]{1,0:T(8,128)(2,1)} %x_ref.1, bf16[256,4096]{1,0:T(8,128)(2,1)} %y_ref.1, bf16[8,2,128,128]{3,2,1,0:T(8,128)(2,1)} %bitcast.19), custom_call_target="tpu_custom_call" | custom-call | tf_op jit(solution)/shard_map/project/pallas_call | solution.py:75
  2.7 13.5 %all_to_all.40.parts_ref = bf16[4,2,64,256]{3,2,1,0:T(8,128)(2,1)S(1)} all-to-all(bf16[4,2,64,256]{3,2,1,0:T(8,128)(2,1)S(1)} %project.1), channel_id=1, replica_groups=mesh['zh'=4,'core'=2,'zl'=2,'xh'=2,'xl'=2,'y'=8] {'zl','xh'}, dimensions={0} | all-to-all | bytes 524288 | tf_op jit(solution)/shard_map/all_to_all | solution.py:207
  16.2 0.8 shard_map.48
  17.0 5.3 %all-to-all-start.2 = ((bf16[8,2,64,256]{3,2,1,0:T(8,128)(2,1)}), bf16[8,2,64,256]{3,2,1,0:T(8,128)(2,1)S(1)}, u32[]{:S(2)}, u32[]{:S(2)}) async-start(bf16[8,2,64,256]{3,2,1,0:T(8,128)(2,1)} %get-tuple-element.19), calls=%async_computation.2 | async-start | bytes 1048576 | tf_op jit(solution)/shard_map/all_to_all | solution.py:212
  22.3 0.8 shard_map.49
  23.1 15.5 %all-to-all-done.2.a_ref = bf16[8,2,64,256]{3,2,1,0:T(8,128)(2,1)S(1)} async-done(((bf16[8,2,64,256]{3,2,1,0:T(8,128)(2,1)}), bf16[8,2,64,256]{3,2,1,0:T(8,128)(2,1)S(1)}, u32[]{:S(2)}, u32[]{:S(2)}) %all-to-all-start.2) | async-done | bytes 524320 | tf_op jit(solution)/shard_map/all_to_all | solution.py:212
  38.6 4.3 %all-to-all-start.1 = ((bf16[16,2,32,256]{3,2,1,0:T(8,128)(2,1)}), bf16[16,2,32,256]{3,2,1,0:T(8,128)(2,1)S(1)}, u32[]{:S(2)}, u32[]{:S(2)}) async-start(bf16[16,2,32,256]{3,2,1,0:T(8,128)(2,1)} %shard_map.49), calls=%async_computation.1 | async-start | bytes 1048576 | tf_op jit(solution)/shard_map/all_to_all | solution.py:225
  42.9 2.1 %collective-permute-start.3 = (bf16[8,2,64,256]{3,2,1,0:T(8,128)(2,1)S(1)}, bf16[8,2,64,256]{3,2,1,0:T(8,128)(2,1)S(1)}, u32[]{:S(2)}, u32[]{:S(2)}) collective-permute-start(bf16[8,2,64,256]{3,2,1,0:T(8,128)(2,1)S(1)} %all-to-all-done.2.a_ref), channel_id=1, source_target_pairs={{0,64},{64,0},{1,65},{65,1},{2,66},{66,2},{3,67},{67,3},{4,68},{68... | collective-permute-start | bytes 1572872 | tf_op jit(solution)/shard_map/ppermute | solution.py:226
  45.0 8.4 %all-to-all-done.1 = bf16[16,2,32,256]{3,2,1,0:T(8,128)(2,1)S(1)} async-done(((bf16[16,2,32,256]{3,2,1,0:T(8,128)(2,1)}), bf16[16,2,32,256]{3,2,1,0:T(8,128)(2,1)S(1)}, u32[]{:S(2)}, u32[]{:S(2)}) %all-to-all-start.1) | async-done | bytes 524320 | tf_op jit(solution)/shard_map/all_to_all | solution.py:225
  53.4 1.2 shard_map.50
  54.6 9.5 %all-to-all-start.3 = ((bf16[4,64,512]{2,1,0:T(8,128)(2,1)}), bf16[4,64,512]{2,1,0:T(8,128)(2,1)S(1)}, u32[]{:S(2)}, u32[]{:S(2)}) async-start(bf16[4,64,512]{2,1,0:T(8,128)(2,1)} %shard_map.50), calls=%async_computation.3 | async-start | bytes 524288 | tf_op jit(solution)/shard_map/all_to_all | solution.py:231
  64.7 10.2 %all-to-all-done.3.parts_ref = bf16[4,64,512]{2,1,0:T(8,128)(2,1)S(1)} async-done(((bf16[4,64,512]{2,1,0:T(8,128)(2,1)}), bf16[4,64,512]{2,1,0:T(8,128)(2,1)S(1)}, u32[]{:S(2)}, u32[]{:S(2)}) %all-to-all-start.3) | async-done | bytes 262176 | tf_op jit(solution)/shard_map/all_to_all | solution.py:231
  75.1 12.1 %all_to_all.41.half_ref = bf16[4,64,512]{2,1,0:T(8,128)(2,1)S(1)} all-to-all(bf16[4,64,512]{2,1,0:T(8,128)(2,1)S(1)} %shard_map.52), channel_id=1, replica_groups=mesh['zh'=4,'core'=2,'zl'=2,'xh'=2,'xl'=2,'y'=8] {'zh'}, dimensions={0} | all-to-all | bytes 524288 | tf_op jit(solution)/shard_map/all_to_all | solution.py:235
  87.1 1.0 shard_map.53
  88.1 4.7 %all-to-all-start.5 = ((bf16[16,32,256]{2,1,0:T(8,128)(2,1)}), bf16[16,32,256]{2,1,0:T(8,128)(2,1)S(1)}, u32[]{:S(2)}, u32[]{:S(2)}) async-start(bf16[16,32,256]{2,1,0:T(8,128)(2,1)} %bitcast.11), calls=%async_computation.5 | async-start | bytes 524288 | tf_op jit(solution)/shard_map/all_to_all | solution.py:237
  92.9 2.1 %collective-permute-start = (bf16[4,2,128,128]{3,2,1,0:T(8,128)(2,1)S(1)}, bf16[4,2,128,128]{3,2,1,0:T(8,128)(2,1)S(1)}, u32[]{:S(2)}, u32[]{:S(2)}) collective-permute-start(bf16[4,2,128,128]{3,2,1,0:T(8,128)(2,1)S(1)} %get-tuple-element.23), channel_id=1, source_target_pairs={{0,32},{32,0},{1,33},{33,1},{2,34},{34,2},{3,35},{35,3},{4,36},{36... | collective-permute-start | bytes 786440 | tf_op jit(solution)/shard_map/ppermute | solution.py:215
  94.9 8.1 %collective-permute-done.came_ref = bf16[4,2,128,128]{3,2,1,0:T(8,128)(2,1)S(1)} collective-permute-done((bf16[4,2,128,128]{3,2,1,0:T(8,128)(2,1)S(1)}, bf16[4,2,128,128]{3,2,1,0:T(8,128)(2,1)S(1)}, u32[]{:S(2)}, u32[]{:S(2)}) %collective-permute-start) | collective-permute-done | bytes 262176 | tf_op jit(solution)/shard_map/ppermute | solution.py:215
  103.1 3.4 %collective-permute-start.1 = (bf16[2,2,2,128,128]{4,3,2,1,0:T(8,128)(2,1)S(1)}, bf16[2,2,2,128,128]{4,3,2,1,0:T(8,128)(2,1)S(1)}, u32[]{:S(2)}, u32[]{:S(2)}) collective-permute-start(bf16[2,2,2,128,128]{4,3,2,1,0:T(8,128)(2,1)S(1)} %get-tuple-element.15), channel_id=1, source_target_pairs={{0,8},{8,0},{1,9},{9,1},{2,10},{10,2},{3,11},{11,3},{4,12},{12,4},... | collective-permute-start | bytes 786440 | tf_op jit(solution)/shard_map/ppermute | solution.py:218
  106.5 0.8 shard_map.54
  107.3 5.4 %all-to-all-start.6 = ((bf16[8,64,256]{2,1,0:T(8,128)(2,1)}), bf16[8,64,256]{2,1,0:T(8,128)(2,1)S(1)}, u32[]{:S(2)}, u32[]{:S(2)}) async-start(bf16[8,64,256]{2,1,0:T(8,128)(2,1)} %shard_map.54), calls=%async_computation.6 | async-start | bytes 524288 | tf_op jit(solution)/shard_map/all_to_all | solution.py:244
  112.8 4.9 %collective-permute-start.2 = (bf16[2,2,2,128,128]{4,3,2,1,0:T(8,128)(2,1)S(1)}, bf16[2,2,2,128,128]{4,3,2,1,0:T(8,128)(2,1)S(1)}, u32[]{:S(2)}, u32[]{:S(2)}) collective-permute-start(bf16[2,2,2,128,128]{4,3,2,1,0:T(8,128)(2,1)S(1)} %get-tuple-element.17), channel_id=1, source_target_pairs={{0,16},{16,0},{1,17},{17,1},{2,18},{18,2},{3,19},{19,3},{4,20},{20... | collective-permute-start | bytes 786440 | tf_op jit(solution)/shard_map/ppermute | solution.py:233
  117.7 6.7 %collective-permute-done.2.came_ref = bf16[2,2,2,128,128]{4,3,2,1,0:T(8,128)(2,1)S(1)} collective-permute-done((bf16[2,2,2,128,128]{4,3,2,1,0:T(8,128)(2,1)S(1)}, bf16[2,2,2,128,128]{4,3,2,1,0:T(8,128)(2,1)S(1)}, u32[]{:S(2)}, u32[]{:S(2)}) %collective-permute-start.2) | collective-permute-done | bytes 262176 | tf_op jit(solution)/shard_map/ppermute | solution.py:233
  124.8 13.9 %all_to_all.42 = bf16[8,64,256]{2,1,0:T(8,128)(2,1)S(1)} all-to-all(bf16[8,64,256]{2,1,0:T(8,128)(2,1)S(1)} %shard_map.55), channel_id=1, replica_groups=mesh['zh'=4,'core'=2,'zl'=2,'xh'=2,'xl'=2,'y'=8] {'y'}, dimensions={0} | all-to-all | bytes 524288 | tf_op jit(solution)/shard_map/all_to_all | solution.py:251
  138.7 0.7 reduce_sum.12
  (25 shorter events, 1.1 us)
Async XLA Ops:
  17.0 21.6 %all-to-all-start.2 = ((bf16[8,2,64,256]{3,2,1,0:T(8,128)(2,1)}), bf16[8,2,64,256]{3,2,1,0:T(8,128)(2,1)S(1)}, u32[]{:S(2)}, u32[]{:S(2)}) async-start(bf16[8,2,64,256]{3,2,1,0:T(8,128)(2,1)} %get-tuple-element.19), calls=%async_computation.2 | async-start | bytes 1048576 | tf_op jit(solution)/shard_map/all_to_all | solution.py:212
  22.3 41.9 %copy-start.1 = (f32[4096]{0:T(1024)S(1)}, f32[4096]{0:T(1024)}, u32[]{:S(2)}) copy-start(f32[4096]{0:T(1024)} %param.7) | copy-start | bytes 49156
  38.6 14.8 %all-to-all-start.1 = ((bf16[16,2,32,256]{3,2,1,0:T(8,128)(2,1)}), bf16[16,2,32,256]{3,2,1,0:T(8,128)(2,1)S(1)}, u32[]{:S(2)}, u32[]{:S(2)}) async-start(bf16[16,2,32,256]{3,2,1,0:T(8,128)(2,1)} %shard_map.49), calls=%async_computation.1 | async-start | bytes 1048576 | tf_op jit(solution)/shard_map/all_to_all | solution.py:225
  42.9 10.5 %collective-permute-start.3 = (bf16[8,2,64,256]{3,2,1,0:T(8,128)(2,1)S(1)}, bf16[8,2,64,256]{3,2,1,0:T(8,128)(2,1)S(1)}, u32[]{:S(2)}, u32[]{:S(2)}) collective-permute-start(bf16[8,2,64,256]{3,2,1,0:T(8,128)(2,1)S(1)} %all-to-all-done.2.a_ref), channel_id=1, source_target_pairs={{0,64},{64,0},{1,65},{65,1},{2,66},{66,2},{3,67},{67,3},{4,68},{68... | collective-permute-start | bytes 1572872 | tf_op jit(solution)/shard_map/ppermute | solution.py:226
  54.6 38.2 %copy-start = (bf16[1,8,2,128,128]{4,3,2,1,0:T(8,128)(2,1)S(1)}, bf16[1,8,2,128,128]{4,3,2,1,0:T(8,128)(2,1)}, u32[]{:S(2)}) copy-start(bf16[1,8,2,128,128]{4,3,2,1,0:T(8,128)(2,1)} %param.6) | copy-start | bytes 1572868
  54.6 20.3 %all-to-all-start.3 = ((bf16[4,64,512]{2,1,0:T(8,128)(2,1)}), bf16[4,64,512]{2,1,0:T(8,128)(2,1)S(1)}, u32[]{:S(2)}, u32[]{:S(2)}) async-start(bf16[4,64,512]{2,1,0:T(8,128)(2,1)} %shard_map.50), calls=%async_computation.3 | async-start | bytes 524288 | tf_op jit(solution)/shard_map/all_to_all | solution.py:231
  88.1 18.4 %all-to-all-start.5 = ((bf16[16,32,256]{2,1,0:T(8,128)(2,1)}), bf16[16,32,256]{2,1,0:T(8,128)(2,1)S(1)}, u32[]{:S(2)}, u32[]{:S(2)}) async-start(bf16[16,32,256]{2,1,0:T(8,128)(2,1)} %bitcast.11), calls=%async_computation.5 | async-start | bytes 524288 | tf_op jit(solution)/shard_map/all_to_all | solution.py:237
  92.9 10.2 %collective-permute-start = (bf16[4,2,128,128]{3,2,1,0:T(8,128)(2,1)S(1)}, bf16[4,2,128,128]{3,2,1,0:T(8,128)(2,1)S(1)}, u32[]{:S(2)}, u32[]{:S(2)}) collective-permute-start(bf16[4,2,128,128]{3,2,1,0:T(8,128)(2,1)S(1)} %get-tuple-element.23), channel_id=1, source_target_pairs={{0,32},{32,0},{1,33},{33,1},{2,34},{34,2},{3,35},{35,3},{4,36},{36... | collective-permute-start | bytes 786440 | tf_op jit(solution)/shard_map/ppermute | solution.py:215
  103.1 9.6 %collective-permute-start.1 = (bf16[2,2,2,128,128]{4,3,2,1,0:T(8,128)(2,1)S(1)}, bf16[2,2,2,128,128]{4,3,2,1,0:T(8,128)(2,1)S(1)}, u32[]{:S(2)}, u32[]{:S(2)}) collective-permute-start(bf16[2,2,2,128,128]{4,3,2,1,0:T(8,128)(2,1)S(1)} %get-tuple-element.15), channel_id=1, source_target_pairs={{0,8},{8,0},{1,9},{9,1},{2,10},{10,2},{3,11},{11,3},{4,12},{12,4},... | collective-permute-start | bytes 786440 | tf_op jit(solution)/shard_map/ppermute | solution.py:218
  107.3 17.1 %all-to-all-start.6 = ((bf16[8,64,256]{2,1,0:T(8,128)(2,1)}), bf16[8,64,256]{2,1,0:T(8,128)(2,1)S(1)}, u32[]{:S(2)}, u32[]{:S(2)}) async-start(bf16[8,64,256]{2,1,0:T(8,128)(2,1)} %shard_map.54), calls=%async_computation.6 | async-start | bytes 524288 | tf_op jit(solution)/shard_map/all_to_all | solution.py:244
  112.8 11.6 %collective-permute-start.2 = (bf16[2,2,2,128,128]{4,3,2,1,0:T(8,128)(2,1)S(1)}, bf16[2,2,2,128,128]{4,3,2,1,0:T(8,128)(2,1)S(1)}, u32[]{:S(2)}, u32[]{:S(2)}) collective-permute-start(bf16[2,2,2,128,128]{4,3,2,1,0:T(8,128)(2,1)S(1)} %get-tuple-element.17), channel_id=1, source_target_pairs={{0,16},{16,0},{1,17},{17,1},{2,18},{18,2},{3,19},{19,3},{4,20},{20... | collective-permute-start | bytes 786440 | tf_op jit(solution)/shard_map/ppermute | solution.py:233

commit v2 on v1

--- a/solution.py
+++ b/solution.py
@@ -87,7 +87,7 @@
     )(inputs, upstream, eig)
 
 
-def spread_kernel(parts_ref, own_ref, copies_ref):
+def spread_kernel(parts_ref, own_ref, halves_ref, copies_ref):
     total = parts_ref[0].astype(F32)
     for k in range(1, parts_ref.shape[0]):
         total += parts_ref[k].astype(F32)
@@ -95,27 +95,36 @@
     own_ref[...] = own
     for k in range(copies_ref.shape[0]):
         copies_ref[k] = own
-
-
-def again_kernel(own_ref, out_ref):
     for core in range(2):
         for k in range(8):
-            out_ref[core * 8 + k] = own_ref[:, core * 32 : core * 32 + 32]
-
-
-def gram_kernel(b_ref, a_ref, other_ref, out_ref):
+            halves_ref[core * 8 + k] = own[:, core * 32 : core * 32 + 32]
+
+
+def gram_own_kernel(b_ref, a_ref, out_ref):
+    tokens = a_ref.shape[3]
     core = lax.axis_index("core")
+    out_ref[...] = gram_part(b_ref, core, a_ref, tokens)
+
+
+def gram_other_kernel(b_ref, a_ref, first_ref, out_ref):
     tokens = a_ref.shape[3]
-    block = jnp.zeros(out_ref.shape, F32).reshape(256, -1)
-    for of, ref in ((core, a_ref), (core ^ 1, other_ref)):
-        for s in range(2):
-            block += lax.dot_general(
-                b_ref[of, :, s].reshape(256, tokens),
-                ref[:, 1 - s].reshape(-1, tokens),
-                (((1,), (1,)), ((), ())),
-                preferred_element_type=F32,
-            )
+    core = lax.axis_index("core")
+    block = first_ref[...] + gram_part(b_ref, core ^ 1, a_ref, tokens)
     out_ref[...] = block.astype(BF16).reshape(out_ref.shape)
+
+
+def gram_part(b_ref, of, a_ref, tokens):
+    over = (((1,), (1,)), ((), ()))
+    part = [
+        lax.dot_general(
+            b_ref[of, :, s].reshape(256, tokens),
+            a_ref[:, 1 - s].reshape(-1, tokens),
+            over,
+            preferred_element_type=F32,
+        )
+        for s in range(2)
+    ]
+    return part[0] + part[1]
 
 
 def roots_kernel(*refs):
@@ -205,9 +214,17 @@
 
     parts = project(inputs, upstream, eig)
     got = lax.all_to_all(parts, ROWS, 0, 0, tiled=True)
-    own, copies = call(
-        spread_kernel, (got,), (out(BF16, 2, 64, tokens), out(BF16, 8, 2, 64, tokens))
-    )
+    own, pieces, copies = call(
+        spread_kernel,
+        (got,),
+        (
+            out(BF16, 2, 64, tokens),
+            out(BF16, 16, 2, 32, tokens),
+            out(BF16, 8, 2, 64, tokens),
+        ),
+    )
+    left = lax.all_to_all(pieces, ("core", *COLS), 0, 0, tiled=True)
+    left = left.reshape(2, 8, 2, 32, tokens)
     halves = eig.reshape(2, 4, 2, 128, 128)
     right = lax.all_to_all(copies, "y", 0, 0, tiled=True)
     away = lax.dynamic_index_in_dim(halves, 1 - zl, 0, keepdims=False)
@@ -221,12 +238,9 @@
         (lam_rows, lam_cols, lam_own),
         (out(F32, 64, 1), out(F32, 1, 512), out(F32, 64, 1)),
     )
-    again = call(again_kernel, (own,), out(BF16, 16, 2, 32, tokens))
-    left = lax.all_to_all(again, ("core", *COLS), 0, 0, tiled=True)
     other = lax.ppermute(right, "core", SWAP)
-    both = call(
-        gram_kernel, (left.reshape(2, 8, 2, 32, tokens), right, other), out(BF16, 4, 64, 512)
-    )
+    first = call(gram_own_kernel, (left, right), out(F32, 256, 512))
+    both = call(gram_other_kernel, (left, other, first), out(BF16, 4, 64, 512))
 
     shares = lax.all_to_all(both, "zh", 0, 0, tiled=True)
     keep_h, send_h = call(split_h_kernel, (keep_l, got_l), (quarter, quarter))

time: 140 us -> 140 us (level)
  blocking collectives: 39.4 us -> 60.9 us
  waiting for transfers between devices: 49.1 us -> 33.5 us
  starting transfers between devices: 41.6 us -> 36.3 us
    all_to_all x0 -> x1, blocking collectives: none -> 21.4 us  [on_device(): right = lax.all_to_all(copies, 'y', 0, 0, tiled=True)]
    all_to_all x2 -> x1, waiting for transfers between devices: 23.9 us -> 8.41 us  [on_device(): left = lax.all_to_all(pieces, ('core', *COLS), 0, 0, tiled=True)]
    all_to_all x2 -> x1, starting transfers between devices: 9.56 us -> 4.28 us  [on_device(): left = lax.all_to_all(pieces, ('core', *COLS), 0, 0, tiled=True)]
  transfers between devices with their start and end apart: 9 -> 8, of which waited for: 5 -> 4; matrix products, arithmetic and copies ran while one was open for 0% -> 0% of each run, Pallas kernels for 1% -> 1%
where the time goes in v2:
time: 140 us; the launch traced here: 139 us
  blocking collectives  60.9 us (44%)
  starting transfers between devices  36.3 us (26%)
  waiting for transfers between devices  33.5 us (24%)
  Pallas kernels  7.27 us (5%)
    all_to_all x1, blocking collectives, on_device(): right = lax.all_to_all(copies, 'y', 0, 0, tiled=True)  21.4 us
    all_to_all x1, blocking collectives, on_device(): blocks = lax.all_to_all(grad_part, 'y', 0, 0, tiled=True)  13.9 us
    all_to_all x1, blocking collectives, on_device(): got = lax.all_to_all(parts, ROWS, 0, 0, tiled=True)  13.5 us
    all_to_all x1, blocking collectives, on_device(): mine = lax.all_to_all(part, 'zh', 0, 0, tiled=True)  12.1 us
    all_to_all x1, waiting for transfers between devices, on_device(): shares = lax.all_to_all(both, 'zh', 0, 0, tiled=True)  10.2 us
    all_to_all x1, starting transfers between devices, on_device(): shares = lax.all_to_all(both, 'zh', 0, 0, tiled=True)  9.53 us
    all_to_all x1, waiting for transfers between devices, on_device(): left = lax.all_to_all(pieces, ('core', *COLS), 0, 0, tiled=True)  8.41 us
    ppermute x1, waiting for transfers between devices, on_device(): came = lax.ppermute(away, 'zl', SWAP)  8.14 us
  transfers between devices with their start and end apart: 8, of which 4 were waited for; matrix products, arithmetic and copies ran while one was open for 0% of the time, Pallas kernels for 1%

profile of v2, /device:TPU:64, one launch (start us, length us, event | category | flops | bytes accessed | tf_op | source)
XLA Modules:
  0.0 139.4 jit_solution(10805023829996947102)
XLA Ops:
  0.0 2.7 %project.1 = bf16[4,2,64,256]{3,2,1,0:T(8,128)(2,1)S(1)} custom-call(bf16[256,4096]{1,0:T(8,128)(2,1)} %x_ref.1, bf16[256,4096]{1,0:T(8,128)(2,1)} %y_ref.1, bf16[8,2,128,128]{3,2,1,0:T(8,128)(2,1)} %bitcast.20), custom_call_target="tpu_custom_call" | custom-call | tf_op jit(solution)/shard_map/project/pallas_call | solution.py:75
  2.7 13.5 %all_to_all.40.parts_ref = bf16[4,2,64,256]{3,2,1,0:T(8,128)(2,1)S(1)} all-to-all(bf16[4,2,64,256]{3,2,1,0:T(8,128)(2,1)S(1)} %project.1), channel_id=1, replica_groups=mesh['zh'=4,'core'=2,'zl'=2,'xh'=2,'xl'=2,'y'=8] {'zl','xh'}, dimensions={0} | all-to-all | bytes 524288 | tf_op jit(solution)/shard_map/all_to_all | solution.py:216
  16.2 0.9 shard_map.48
  17.1 21.4 %all_to_all.41.a_ref = bf16[8,2,64,256]{3,2,1,0:T(8,128)(2,1)S(1)} all-to-all(bf16[8,2,64,256]{3,2,1,0:T(8,128)(2,1)S(1)} %get-tuple-element.20), channel_id=1, replica_groups=mesh['zh'=4,'core'=2,'zl'=2,'xh'=2,'xl'=2,'y'=8] {'y'}, dimensions={0} | all-to-all | bytes 1048576 | tf_op jit(solution)/shard_map/all_to_all | solution.py:229
  38.5 4.3 %all-to-all-start.1 = ((bf16[16,2,32,256]{3,2,1,0:T(8,128)(2,1)}), bf16[16,2,32,256]{3,2,1,0:T(8,128)(2,1)S(1)}, u32[]{:S(2)}, u32[]{:S(2)}) async-start(bf16[16,2,32,256]{3,2,1,0:T(8,128)(2,1)} %get-tuple-element.19), calls=%async_computation.1 | async-start | bytes 1048576 | tf_op jit(solution)/shard_map/all_to_all | solution.py:226
  42.8 2.1 %collective-permute-start.3 = (bf16[8,2,64,256]{3,2,1,0:T(8,128)(2,1)S(1)}, bf16[8,2,64,256]{3,2,1,0:T(8,128)(2,1)S(1)}, u32[]{:S(2)}, u32[]{:S(2)}) collective-permute-start(bf16[8,2,64,256]{3,2,1,0:T(8,128)(2,1)S(1)} %all_to_all.41.a_ref), channel_id=1, source_target_pairs={{0,64},{64,0},{1,65},{65,1},{2,66},{66,2},{3,67},{67,3},{4,68},{68... | collective-permute-start | bytes 1572872 | tf_op jit(solution)/shard_map/ppermute | solution.py:241
  44.9 8.4 %all-to-all-done.1 = bf16[16,2,32,256]{3,2,1,0:T(8,128)(2,1)S(1)} async-done(((bf16[16,2,32,256]{3,2,1,0:T(8,128)(2,1)}), bf16[16,2,32,256]{3,2,1,0:T(8,128)(2,1)S(1)}, u32[]{:S(2)}, u32[]{:S(2)}) %all-to-all-start.1) | async-done | bytes 524320 | tf_op jit(solution)/shard_map/all_to_all | solution.py:226
  53.3 0.3 shard_map.49.first_ref
  53.6 1.0 shard_map.50
  54.7 9.5 %all-to-all-start.3 = ((bf16[4,64,512]{2,1,0:T(8,128)(2,1)}), bf16[4,64,512]{2,1,0:T(8,128)(2,1)S(1)}, u32[]{:S(2)}, u32[]{:S(2)}) async-start(bf16[4,64,512]{2,1,0:T(8,128)(2,1)} %shard_map.50), calls=%async_computation.3 | async-start | bytes 524288 | tf_op jit(solution)/shard_map/all_to_all | solution.py:245
  64.8 10.2 %all-to-all-done.3.parts_ref = bf16[4,64,512]{2,1,0:T(8,128)(2,1)S(1)} async-done(((bf16[4,64,512]{2,1,0:T(8,128)(2,1)}), bf16[4,64,512]{2,1,0:T(8,128)(2,1)S(1)}, u32[]{:S(2)}, u32[]{:S(2)}) %all-to-all-start.3) | async-done | bytes 262176 | tf_op jit(solution)/shard_map/all_to_all | solution.py:245
  75.1 12.1 %all_to_all.42.half_ref = bf16[4,64,512]{2,1,0:T(8,128)(2,1)S(1)} all-to-all(bf16[4,64,512]{2,1,0:T(8,128)(2,1)S(1)} %shard_map.52), channel_id=1, replica_groups=mesh['zh'=4,'core'=2,'zl'=2,'xh'=2,'xl'=2,'y'=8] {'zh'}, dimensions={0} | all-to-all | bytes 524288 | tf_op jit(solution)/shard_map/all_to_all | solution.py:249
  87.2 1.0 shard_map.53
  88.2 4.7 %all-to-all-start.5 = ((bf16[16,32,256]{2,1,0:T(8,128)(2,1)}), bf16[16,32,256]{2,1,0:T(8,128)(2,1)S(1)}, u32[]{:S(2)}, u32[]{:S(2)}) async-start(bf16[16,32,256]{2,1,0:T(8,128)(2,1)} %bitcast.11), calls=%async_computation.5 | async-start | bytes 524288 | tf_op jit(solution)/shard_map/all_to_all | solution.py:251
  92.9 2.1 %collective-permute-start = (bf16[4,2,128,128]{3,2,1,0:T(8,128)(2,1)S(1)}, bf16[4,2,128,128]{3,2,1,0:T(8,128)(2,1)S(1)}, u32[]{:S(2)}, u32[]{:S(2)}) collective-permute-start(bf16[4,2,128,128]{3,2,1,0:T(8,128)(2,1)S(1)} %get-tuple-element.25), channel_id=1, source_target_pairs={{0,32},{32,0},{1,33},{33,1},{2,34},{34,2},{3,35},{35,3},{4,36},{36... | collective-permute-start | bytes 786440 | tf_op jit(solution)/shard_map/ppermute | solution.py:232
  95.0 8.1 %collective-permute-done.came_ref = bf16[4,2,128,128]{3,2,1,0:T(8,128)(2,1)S(1)} collective-permute-done((bf16[4,2,128,128]{3,2,1,0:T(8,128)(2,1)S(1)}, bf16[4,2,128,128]{3,2,1,0:T(8,128)(2,1)S(1)}, u32[]{:S(2)}, u32[]{:S(2)}) %collective-permute-start) | collective-permute-done | bytes 262176 | tf_op jit(solution)/shard_map/ppermute | solution.py:232
  103.2 3.4 %collective-permute-start.1 = (bf16[2,2,2,128,128]{4,3,2,1,0:T(8,128)(2,1)S(1)}, bf16[2,2,2,128,128]{4,3,2,1,0:T(8,128)(2,1)S(1)}, u32[]{:S(2)}, u32[]{:S(2)}) collective-permute-start(bf16[2,2,2,128,128]{4,3,2,1,0:T(8,128)(2,1)S(1)} %get-tuple-element.16), channel_id=1, source_target_pairs={{0,8},{8,0},{1,9},{9,1},{2,10},{10,2},{3,11},{11,3},{4,12},{12,4},... | collective-permute-start | bytes 786440 | tf_op jit(solution)/shard_map/ppermute | solution.py:235
  106.6 0.8 shard_map.54
  107.4 5.4 %all-to-all-start.6 = ((bf16[8,64,256]{2,1,0:T(8,128)(2,1)}), bf16[8,64,256]{2,1,0:T(8,128)(2,1)S(1)}, u32[]{:S(2)}, u32[]{:S(2)}) async-start(bf16[8,64,256]{2,1,0:T(8,128)(2,1)} %shard_map.54), calls=%async_computation.6 | async-start | bytes 524288 | tf_op jit(solution)/shard_map/all_to_all | solution.py:258
  112.8 4.9 %collective-permute-start.2 = (bf16[2,2,2,128,128]{4,3,2,1,0:T(8,128)(2,1)S(1)}, bf16[2,2,2,128,128]{4,3,2,1,0:T(8,128)(2,1)S(1)}, u32[]{:S(2)}, u32[]{:S(2)}) collective-permute-start(bf16[2,2,2,128,128]{4,3,2,1,0:T(8,128)(2,1)S(1)} %get-tuple-element.18), channel_id=1, source_target_pairs={{0,16},{16,0},{1,17},{17,1},{2,18},{18,2},{3,19},{19,3},{4,20},{20... | collective-permute-start | bytes 786440 | tf_op jit(solution)/shard_map/ppermute | solution.py:247
  117.7 6.7 %collective-permute-done.2.came_ref = bf16[2,2,2,128,128]{4,3,2,1,0:T(8,128)(2,1)S(1)} collective-permute-done((bf16[2,2,2,128,128]{4,3,2,1,0:T(8,128)(2,1)S(1)}, bf16[2,2,2,128,128]{4,3,2,1,0:T(8,128)(2,1)S(1)}, u32[]{:S(2)}, u32[]{:S(2)}) %collective-permute-start.2) | collective-permute-done | bytes 262176 | tf_op jit(solution)/shard_map/ppermute | solution.py:247
  124.5 0.3 shard_map.55
  124.8 13.9 %all_to_all.43 = bf16[8,64,256]{2,1,0:T(8,128)(2,1)S(1)} all-to-all(bf16[8,64,256]{2,1,0:T(8,128)(2,1)S(1)} %shard_map.55), channel_id=1, replica_groups=mesh['zh'=4,'core'=2,'zl'=2,'xh'=2,'xl'=2,'y'=8] {'y'}, dimensions={0} | all-to-all | bytes 524288 | tf_op jit(solution)/shard_map/all_to_all | solution.py:265
  138.7 0.7 reduce_sum.12
  (24 shorter events, 0.8 us)
Async XLA Ops:
  38.5 14.8 %all-to-all-start.1 = ((bf16[16,2,32,256]{3,2,1,0:T(8,128)(2,1)}), bf16[16,2,32,256]{3,2,1,0:T(8,128)(2,1)S(1)}, u32[]{:S(2)}, u32[]{:S(2)}) async-start(bf16[16,2,32,256]{3,2,1,0:T(8,128)(2,1)} %get-tuple-element.19), calls=%async_computation.1 | async-start | bytes 1048576 | tf_op jit(solution)/shard_map/all_to_all | solution.py:226
  42.8 21.4 %copy-start.1 = (f32[4096]{0:T(1024)S(1)}, f32[4096]{0:T(1024)}, u32[]{:S(2)}) copy-start(f32[4096]{0:T(1024)} %param.7) | copy-start | bytes 49156
  42.8 10.8 %collective-permute-start.3 = (bf16[8,2,64,256]{3,2,1,0:T(8,128)(2,1)S(1)}, bf16[8,2,64,256]{3,2,1,0:T(8,128)(2,1)S(1)}, u32[]{:S(2)}, u32[]{:S(2)}) collective-permute-start(bf16[8,2,64,256]{3,2,1,0:T(8,128)(2,1)S(1)} %all_to_all.41.a_ref), channel_id=1, source_target_pairs={{0,64},{64,0},{1,65},{65,1},{2,66},{66,2},{3,67},{67,3},{4,68},{68... | collective-permute-start | bytes 1572872 | tf_op jit(solution)/shard_map/ppermute | solution.py:241
  54.7 38.2 %copy-start = (bf16[1,8,2,128,128]{4,3,2,1,0:T(8,128)(2,1)S(1)}, bf16[1,8,2,128,128]{4,3,2,1,0:T(8,128)(2,1)}, u32[]{:S(2)}) copy-start(bf16[1,8,2,128,128]{4,3,2,1,0:T(8,128)(2,1)} %param.6) | copy-start | bytes 1572868
  54.7 20.3 %all-to-all-start.3 = ((bf16[4,64,512]{2,1,0:T(8,128)(2,1)}), bf16[4,64,512]{2,1,0:T(8,128)(2,1)S(1)}, u32[]{:S(2)}, u32[]{:S(2)}) async-start(bf16[4,64,512]{2,1,0:T(8,128)(2,1)} %shard_map.50), calls=%async_computation.3 | async-start | bytes 524288 | tf_op jit(solution)/shard_map/all_to_all | solution.py:245
  88.2 18.4 %all-to-all-start.5 = ((bf16[16,32,256]{2,1,0:T(8,128)(2,1)}), bf16[16,32,256]{2,1,0:T(8,128)(2,1)S(1)}, u32[]{:S(2)}, u32[]{:S(2)}) async-start(bf16[16,32,256]{2,1,0:T(8,128)(2,1)} %bitcast.11), calls=%async_computation.5 | async-start | bytes 524288 | tf_op jit(solution)/shard_map/all_to_all | solution.py:251
  92.9 10.2 %collective-permute-start = (bf16[4,2,128,128]{3,2,1,0:T(8,128)(2,1)S(1)}, bf16[4,2,128,128]{3,2,1,0:T(8,128)(2,1)S(1)}, u32[]{:S(2)}, u32[]{:S(2)}) collective-permute-start(bf16[4,2,128,128]{3,2,1,0:T(8,128)(2,1)S(1)} %get-tuple-element.25), channel_id=1, source_target_pairs={{0,32},{32,0},{1,33},{33,1},{2,34},{34,2},{3,35},{35,3},{4,36},{36... | collective-permute-start | bytes 786440 | tf_op jit(solution)/shard_map/ppermute | solution.py:232
  103.2 9.6 %collective-permute-start.1 = (bf16[2,2,2,128,128]{4,3,2,1,0:T(8,128)(2,1)S(1)}, bf16[2,2,2,128,128]{4,3,2,1,0:T(8,128)(2,1)S(1)}, u32[]{:S(2)}, u32[]{:S(2)}) collective-permute-start(bf16[2,2,2,128,128]{4,3,2,1,0:T(8,128)(2,1)S(1)} %get-tuple-element.16), channel_id=1, source_target_pairs={{0,8},{8,0},{1,9},{9,1},{2,10},{10,2},{3,11},{11,3},{4,12},{12,4},... | collective-permute-start | bytes 786440 | tf_op jit(solution)/shard_map/ppermute | solution.py:235
  107.4 17.1 %all-to-all-start.6 = ((bf16[8,64,256]{2,1,0:T(8,128)(2,1)}), bf16[8,64,256]{2,1,0:T(8,128)(2,1)S(1)}, u32[]{:S(2)}, u32[]{:S(2)}) async-start(bf16[8,64,256]{2,1,0:T(8,128)(2,1)} %shard_map.54), calls=%async_computation.6 | async-start | bytes 524288 | tf_op jit(solution)/shard_map/all_to_all | solution.py:258
  112.8 11.6 %collective-permute-start.2 = (bf16[2,2,2,128,128]{4,3,2,1,0:T(8,128)(2,1)S(1)}, bf16[2,2,2,128,128]{4,3,2,1,0:T(8,128)(2,1)S(1)}, u32[]{:S(2)}, u32[]{:S(2)}) collective-permute-start(bf16[2,2,2,128,128]{4,3,2,1,0:T(8,128)(2,1)S(1)} %get-tuple-element.18), channel_id=1, source_target_pairs={{0,16},{16,0},{1,17},{17,1},{2,18},{18,2},{3,19},{19,3},{4,20},{20... | collective-permute-start | bytes 786440 | tf_op jit(solution)/shard_map/ppermute | solution.py:247

commit v3 on v1

--- a/solution.py
+++ b/solution.py
@@ -8,9 +8,11 @@
 
 F32 = jnp.float32
 BF16 = jnp.bfloat16
-AXES = ("zh", "core", "zl", "xh", "xl", "y")
-SIZES = (4, 2, 2, 2, 2, 8)
-ROWS = ("zl", "xh")
+AXES = ("zh1", "zh0", "core", "zl", "xh", "xl", "y2", "y1", "y0")
+SIZES = (2,) * 9
+ROWS = ("xh", "zl")
+LINE = ("y0", "y1", "y2")
+DEPTH = ("zh0", "zh1")
 COLS = ("xl", "zl", "xh")
 SWAP = [(0, 1), (1, 0)]
 
@@ -66,7 +68,10 @@
             copy(s, la).wait()
         part = jnp.dot(xs[s], basis, preferred_element_type=F32)
         turned = part.T.astype(BF16)
-        out_ref[:, s] = turned.reshape(out_ref.shape[0], *out_ref.shape[2:])
+        turned = turned.reshape(out_ref.shape[0], *out_ref.shape[2:])
+        for zl in range(2):
+            for xh in range(2):
+                out_ref[xh * 2 + zl, s] = turned[zl * 2 + xh]
 
 
 def project(inputs, upstream, eig):
@@ -184,12 +189,15 @@
         every_ref[...].reshape(512, tokens),
         preferred_element_type=F32,
     )
-    out_ref[...] = part.astype(BF16).reshape(-1, 64, tokens)
+    part = part.astype(BF16).reshape(8, 64, tokens)
+    for y in range(8):
+        out_ref[(y & 1) * 4 + (y & 2) + (y >> 2)] = part[y]
 
 
 def on_device(inputs, upstream, eig_tiles, eigvals):
-    zl, xh, xl, y = (lax.axis_index(a) for a in ("zl", "xh", "xl", "y"))
-    zh, core = lax.axis_index("zh"), lax.axis_index("core")
+    zl, xh, xl, core = (lax.axis_index(a) for a in ("zl", "xh", "xl", "core"))
+    y = lax.axis_index(("y2", "y1", "y0"))
+    share = lax.axis_index(DEPTH)
     tokens = inputs.shape[0]
     eig = eig_tiles[0]
     r = zl * 2 + xh
@@ -200,8 +208,8 @@
     lam_a = lax.dynamic_index_in_dim(cube, r * 2 + xl, 0, keepdims=False)
     lam_own = lax.dynamic_index_in_dim(lam_a, y, 0, keepdims=False).reshape(64, 1)
     by_core = lax.dynamic_index_in_dim(lam_b.reshape(4, 2, 2, 32), core, 2, keepdims=False)
-    lam_rows = lax.dynamic_index_in_dim(by_core, zh, 0, keepdims=False).reshape(64, 1)
-    lam_cols = lam_a.reshape(1, 512)
+    lam_rows = lax.dynamic_index_in_dim(by_core, share, 0, keepdims=False).reshape(64, 1)
+    lam_cols = jnp.transpose(lam_a.reshape(2, 2, 2, 64), (2, 1, 0, 3)).reshape(1, 512)
 
     parts = project(inputs, upstream, eig)
     got = lax.all_to_all(parts, ROWS, 0, 0, tiled=True)
@@ -209,7 +217,7 @@
         spread_kernel, (got,), (out(BF16, 2, 64, tokens), out(BF16, 8, 2, 64, tokens))
     )
     halves = eig.reshape(2, 4, 2, 128, 128)
-    right = lax.all_to_all(copies, "y", 0, 0, tiled=True)
+    right = lax.all_to_all(copies, LINE, 0, 0, tiled=True)
     away = lax.dynamic_index_in_dim(halves, 1 - zl, 0, keepdims=False)
     kept = lax.dynamic_index_in_dim(halves, zl, 0, keepdims=False)
     came = lax.ppermute(away, "zl", SWAP)
@@ -228,11 +236,11 @@
         gram_kernel, (left.reshape(2, 8, 2, 32, tokens), right, other), out(BF16, 4, 64, 512)
     )
 
-    shares = lax.all_to_all(both, "zh", 0, 0, tiled=True)
+    shares = lax.all_to_all(both, DEPTH, 0, 0, tiled=True)
     keep_h, send_h = call(split_h_kernel, (keep_l, got_l), (quarter, quarter))
     got_h = lax.ppermute(send_h, "xh", SWAP)
     part = call(weigh_kernel, (shares, s_rows, s_cols), out(BF16, 4, 64, 512))
-    mine = lax.all_to_all(part, "zh", 0, 0, tiled=True)
+    mine = lax.all_to_all(part, DEPTH, 0, 0, tiled=True)
     mixed_part = call(mix_kernel, (mine, right, other), out(BF16, 2, 8, 32, tokens))
     mixed = lax.all_to_all(mixed_part.reshape(16, 32, tokens), ("core", *COLS), 0, 0, tiled=True)
     factor = 2.0 / (8 * tokens)
@@ -248,13 +256,13 @@
         out(BF16, 8, 64, tokens),
         (pltpu.VMEM((4, 128, 512), BF16),),
     )
-    blocks = lax.all_to_all(grad_part, "y", 0, 0, tiled=True)
+    blocks = lax.all_to_all(grad_part, LINE, 0, 0, tiled=True)
     return jnp.sum(blocks.astype(F32), 0).astype(BF16)
 
 
 def solution(mesh):
     grid = Mesh(mesh.devices.reshape(SIZES), AXES)
-    dp, mp = AXES[:2], AXES[2:]
+    dp, mp = AXES[:3], AXES[3:]
     return jax.shard_map(
         on_device,
         mesh=grid,

time: 140 us -> 138 us (0.986)
  the two profiles are of different devices: /device:TPU:64 before, /device:TPU:16 now
where the time goes in v3:
time: 138 us
  waiting for transfers between devices  46.9 us (34%)
  starting transfers between devices  43.2 us (31%)
  blocking collectives  38.2 us (28%)
  Pallas kernels  7.85 us (6%)
    all_to_all x1, blocking collectives, on_device(): got = lax.all_to_all(parts, ROWS, 0, 0, tiled=True)  13.1 us
    all_to_all x1, waiting for transfers between devices, on_device(): right = lax.all_to_all(copies, LINE, 0, 0, tiled=True)  13 us
    all_to_all x1, blocking collectives, on_device(): mine = lax.all_to_all(part, DEPTH, 0, 0, tiled=True)  12.8 us
    all_to_all x1, blocking collectives, on_device(): blocks = lax.all_to_all(grad_part, LINE, 0, 0, tiled=True)  12.3 us
    all_to_all x1, waiting for transfers between devices, on_device(): shares = lax.all_to_all(both, DEPTH, 0, 0, tiled=True)  10 us
    all_to_all x1, starting transfers between devices, on_device(): shares = lax.all_to_all(both, DEPTH, 0, 0, tiled=True)  9.53 us
    all_to_all x1, waiting for transfers between devices, on_device(): left = lax.all_to_all(again, ('core', *COLS), 0, 0, tiled=True)  8.47 us
    ppermute x1, waiting for transfers between devices, on_device(): came = lax.ppermute(away, 'zl', SWAP)  7.62 us
  transfers between devices with their start and end apart: 9, of which 6 were waited for; matrix products, arithmetic and copies ran while one was open for 0% of the time, Pallas kernels for 1%

profile of v3, /device:TPU:16, one launch (start us, length us, event | category | flops | bytes accessed | tf_op | source)
XLA Modules:
  0.0 137.6 jit_solution(12313343533593674917)
XLA Ops:
  0.0 2.7 %project.1 = bf16[4,2,64,256]{3,2,1,0:T(8,128)(2,1)S(1)} custom-call(bf16[256,4096]{1,0:T(8,128)(2,1)} %x_ref.1, bf16[256,4096]{1,0:T(8,128)(2,1)} %y_ref.1, bf16[8,2,128,128]{3,2,1,0:T(8,128)(2,1)} %bitcast.22), custom_call_target="tpu_custom_call" | custom-call | tf_op jit(solution)/shard_map/project/pallas_call | solution.py:80
  2.7 13.1 %all_to_all.40.parts_ref = bf16[4,2,64,256]{3,2,1,0:T(8,128)(2,1)S(1)} all-to-all(bf16[4,2,64,256]{3,2,1,0:T(8,128)(2,1)S(1)} %project.1), channel_id=1, replica_groups=mesh['zh1'=2,'zh0'=2,'core'=2,'zl'=2,'xh'=2,'xl'=2,'y2'=2,'y1'=2,'y0'=2]..., dimensions={0} | all-to-all | bytes 524288 | tf_op jit(solution)/shard_map/all_to_all | solution.py:215
  15.8 0.8 shard_map.48
  16.6 7.4 %all-to-all-start.2 = ((bf16[8,2,64,256]{3,2,1,0:T(8,128)(2,1)}), bf16[8,2,64,256]{3,2,1,0:T(8,128)(2,1)S(1)}, u32[]{:S(2)}, u32[]{:S(2)}) async-start(bf16[8,2,64,256]{3,2,1,0:T(8,128)(2,1)} %get-tuple-element.19), calls=%async_computation.2 | async-start | bytes 1048576 | tf_op jit(solution)/shard_map/all_to_all | solution.py:220
  24.1 0.8 shard_map.49
  24.9 13.0 %all-to-all-done.2.a_ref = bf16[8,2,64,256]{3,2,1,0:T(8,128)(2,1)S(1)} async-done(((bf16[8,2,64,256]{3,2,1,0:T(8,128)(2,1)}), bf16[8,2,64,256]{3,2,1,0:T(8,128)(2,1)S(1)}, u32[]{:S(2)}, u32[]{:S(2)}) %all-to-all-start.2) | async-done | bytes 524320 | tf_op jit(solution)/shard_map/all_to_all | solution.py:220
  37.9 3.6 %all-to-all-start.1 = ((bf16[16,2,32,256]{3,2,1,0:T(8,128)(2,1)}), bf16[16,2,32,256]{3,2,1,0:T(8,128)(2,1)S(1)}, u32[]{:S(2)}, u32[]{:S(2)}) async-start(bf16[16,2,32,256]{3,2,1,0:T(8,128)(2,1)} %shard_map.49), calls=%async_computation.1 | async-start | bytes 1048576 | tf_op jit(solution)/shard_map/all_to_all | solution.py:233
  41.5 2.2 %collective-permute-start.3 = (bf16[8,2,64,256]{3,2,1,0:T(8,128)(2,1)S(1)}, bf16[8,2,64,256]{3,2,1,0:T(8,128)(2,1)S(1)}, u32[]{:S(2)}, u32[]{:S(2)}) collective-permute-start(bf16[8,2,64,256]{3,2,1,0:T(8,128)(2,1)S(1)} %all-to-all-done.2.a_ref), channel_id=1, source_target_pairs={{0,64},{64,0},{1,65},{65,1},{2,66},{66,2},{3,67},{67,3},{4,68},{68... | collective-permute-start | bytes 1572872 | tf_op jit(solution)/shard_map/ppermute | solution.py:234
  43.7 8.5 %all-to-all-done.1 = bf16[16,2,32,256]{3,2,1,0:T(8,128)(2,1)S(1)} async-done(((bf16[16,2,32,256]{3,2,1,0:T(8,128)(2,1)}), bf16[16,2,32,256]{3,2,1,0:T(8,128)(2,1)S(1)}, u32[]{:S(2)}, u32[]{:S(2)}) %all-to-all-start.1) | async-done | bytes 524320 | tf_op jit(solution)/shard_map/all_to_all | solution.py:233
  52.2 1.2 shard_map.50
  53.3 9.5 %all-to-all-start.3 = ((bf16[4,64,512]{2,1,0:T(8,128)(2,1)}), bf16[4,64,512]{2,1,0:T(8,128)(2,1)S(1)}, u32[]{:S(2)}, u32[]{:S(2)}) async-start(bf16[4,64,512]{2,1,0:T(8,128)(2,1)} %shard_map.50), calls=%async_computation.3 | async-start | bytes 524288 | tf_op jit(solution)/shard_map/all_to_all | solution.py:239
  63.5 10.0 %all-to-all-done.3.parts_ref = bf16[4,64,512]{2,1,0:T(8,128)(2,1)S(1)} async-done(((bf16[4,64,512]{2,1,0:T(8,128)(2,1)}), bf16[4,64,512]{2,1,0:T(8,128)(2,1)S(1)}, u32[]{:S(2)}, u32[]{:S(2)}) %all-to-all-start.3) | async-done | bytes 262176 | tf_op jit(solution)/shard_map/all_to_all | solution.py:239
  73.6 12.8 %all_to_all.41.half_ref = bf16[4,64,512]{2,1,0:T(8,128)(2,1)S(1)} all-to-all(bf16[4,64,512]{2,1,0:T(8,128)(2,1)S(1)} %shard_map.52), channel_id=1, replica_groups=mesh['zh1'=2,'zh0'=2,'core'=2,'zl'=2,'xh'=2,'xl'=2,'y2'=2,'y1'=2,'y0'=2]..., dimensions={0} | all-to-all | bytes 524288 | tf_op jit(solution)/shard_map/all_to_all | solution.py:243
  86.3 1.0 shard_map.53
  87.4 4.3 %all-to-all-start.5 = ((bf16[16,32,256]{2,1,0:T(8,128)(2,1)}), bf16[16,32,256]{2,1,0:T(8,128)(2,1)S(1)}, u32[]{:S(2)}, u32[]{:S(2)}) async-start(bf16[16,32,256]{2,1,0:T(8,128)(2,1)} %bitcast.13), calls=%async_computation.5 | async-start | bytes 524288 | tf_op jit(solution)/shard_map/all_to_all | solution.py:245
  91.8 3.8 %collective-permute-start = (bf16[4,2,128,128]{3,2,1,0:T(8,128)(2,1)S(1)}, bf16[4,2,128,128]{3,2,1,0:T(8,128)(2,1)S(1)}, u32[]{:S(2)}, u32[]{:S(2)}) collective-permute-start(bf16[4,2,128,128]{3,2,1,0:T(8,128)(2,1)S(1)} %get-tuple-element.23), channel_id=1, source_target_pairs={{0,32},{32,0},{1,33},{33,1},{2,34},{34,2},{3,35},{35,3},{4,36},{36... | collective-permute-start | bytes 786440 | tf_op jit(solution)/shard_map/ppermute | solution.py:223
  95.6 7.6 %collective-permute-done.came_ref = bf16[4,2,128,128]{3,2,1,0:T(8,128)(2,1)S(1)} collective-permute-done((bf16[4,2,128,128]{3,2,1,0:T(8,128)(2,1)S(1)}, bf16[4,2,128,128]{3,2,1,0:T(8,128)(2,1)S(1)}, u32[]{:S(2)}, u32[]{:S(2)}) %collective-permute-start) | collective-permute-done | bytes 262176 | tf_op jit(solution)/shard_map/ppermute | solution.py:223
  103.3 3.4 %collective-permute-start.1 = (bf16[2,2,2,128,128]{4,3,2,1,0:T(8,128)(2,1)S(1)}, bf16[2,2,2,128,128]{4,3,2,1,0:T(8,128)(2,1)S(1)}, u32[]{:S(2)}, u32[]{:S(2)}) collective-permute-start(bf16[2,2,2,128,128]{4,3,2,1,0:T(8,128)(2,1)S(1)} %get-tuple-element.15), channel_id=1, source_target_pairs={{0,8},{8,0},{1,9},{9,1},{2,10},{10,2},{3,11},{11,3},{4,12},{12,4},... | collective-permute-start | bytes 786440 | tf_op jit(solution)/shard_map/ppermute | solution.py:226
  106.6 0.8 shard_map.54
  107.4 4.1 %all-to-all-start.6 = ((bf16[8,64,256]{2,1,0:T(8,128)(2,1)}), bf16[8,64,256]{2,1,0:T(8,128)(2,1)S(1)}, u32[]{:S(2)}, u32[]{:S(2)}) async-start(bf16[8,64,256]{2,1,0:T(8,128)(2,1)} %shard_map.54), calls=%async_computation.6 | async-start | bytes 524288 | tf_op jit(solution)/shard_map/all_to_all | solution.py:252
  111.5 1.5 %collective-permute-done.1.came_ref = bf16[2,2,2,128,128]{4,3,2,1,0:T(8,128)(2,1)S(1)} collective-permute-done((bf16[2,2,2,128,128]{4,3,2,1,0:T(8,128)(2,1)S(1)}, bf16[2,2,2,128,128]{4,3,2,1,0:T(8,128)(2,1)S(1)}, u32[]{:S(2)}, u32[]{:S(2)}) %collective-permute-start.1) | collective-permute-done | bytes 262176 | tf_op jit(solution)/shard_map/ppermute | solution.py:226
  113.0 4.8 %collective-permute-start.2 = (bf16[2,2,2,128,128]{4,3,2,1,0:T(8,128)(2,1)S(1)}, bf16[2,2,2,128,128]{4,3,2,1,0:T(8,128)(2,1)S(1)}, u32[]{:S(2)}, u32[]{:S(2)}) collective-permute-start(bf16[2,2,2,128,128]{4,3,2,1,0:T(8,128)(2,1)S(1)} %get-tuple-element.17), channel_id=1, source_target_pairs={{0,16},{16,0},{1,17},{17,1},{2,18},{18,2},{3,19},{19,3},{4,20},{20... | collective-permute-start | bytes 786440 | tf_op jit(solution)/shard_map/ppermute | solution.py:241
  117.9 6.4 %collective-permute-done.2.came_ref = bf16[2,2,2,128,128]{4,3,2,1,0:T(8,128)(2,1)S(1)} collective-permute-done((bf16[2,2,2,128,128]{4,3,2,1,0:T(8,128)(2,1)S(1)}, bf16[2,2,2,128,128]{4,3,2,1,0:T(8,128)(2,1)S(1)}, u32[]{:S(2)}, u32[]{:S(2)}) %collective-permute-start.2) | collective-permute-done | bytes 262176 | tf_op jit(solution)/shard_map/ppermute | solution.py:241
  124.6 12.3 %all_to_all.42 = bf16[8,64,256]{2,1,0:T(8,128)(2,1)S(1)} all-to-all(bf16[8,64,256]{2,1,0:T(8,128)(2,1)S(1)} %shard_map.55), channel_id=1, replica_groups=mesh['zh1'=2,'zh0'=2,'core'=2,'zl'=2,'xh'=2,'xl'=2,'y2'=2,'y1'=2,'y0'=2]..., dimensions={0} | all-to-all | bytes 524288 | tf_op jit(solution)/shard_map/all_to_all | solution.py:259
  (26 shorter events, 1.8 us)
Async XLA Ops:
  16.6 21.2 %all-to-all-start.2 = ((bf16[8,2,64,256]{3,2,1,0:T(8,128)(2,1)}), bf16[8,2,64,256]{3,2,1,0:T(8,128)(2,1)S(1)}, u32[]{:S(2)}, u32[]{:S(2)}) async-start(bf16[8,2,64,256]{3,2,1,0:T(8,128)(2,1)} %get-tuple-element.19), calls=%async_computation.2 | async-start | bytes 1048576 | tf_op jit(solution)/shard_map/all_to_all | solution.py:220
  24.1 38.8 %copy-start.1 = (f32[4096]{0:T(1024)S(1)}, f32[4096]{0:T(1024)}, u32[]{:S(2)}) copy-start(f32[4096]{0:T(1024)} %param.7) | copy-start | bytes 49156
  37.9 14.3 %all-to-all-start.1 = ((bf16[16,2,32,256]{3,2,1,0:T(8,128)(2,1)}), bf16[16,2,32,256]{3,2,1,0:T(8,128)(2,1)S(1)}, u32[]{:S(2)}, u32[]{:S(2)}) async-start(bf16[16,2,32,256]{3,2,1,0:T(8,128)(2,1)} %shard_map.49), calls=%async_computation.1 | async-start | bytes 1048576 | tf_op jit(solution)/shard_map/all_to_all | solution.py:233
  41.5 10.7 %collective-permute-start.3 = (bf16[8,2,64,256]{3,2,1,0:T(8,128)(2,1)S(1)}, bf16[8,2,64,256]{3,2,1,0:T(8,128)(2,1)S(1)}, u32[]{:S(2)}, u32[]{:S(2)}) collective-permute-start(bf16[8,2,64,256]{3,2,1,0:T(8,128)(2,1)S(1)} %all-to-all-done.2.a_ref), channel_id=1, source_target_pairs={{0,64},{64,0},{1,65},{65,1},{2,66},{66,2},{3,67},{67,3},{4,68},{68... | collective-permute-start | bytes 1572872 | tf_op jit(solution)/shard_map/ppermute | solution.py:234
  53.3 38.4 %copy-start = (bf16[1,8,2,128,128]{4,3,2,1,0:T(8,128)(2,1)S(1)}, bf16[1,8,2,128,128]{4,3,2,1,0:T(8,128)(2,1)}, u32[]{:S(2)}) copy-start(bf16[1,8,2,128,128]{4,3,2,1,0:T(8,128)(2,1)} %param.6) | copy-start | bytes 1572868
  53.3 20.1 %all-to-all-start.3 = ((bf16[4,64,512]{2,1,0:T(8,128)(2,1)}), bf16[4,64,512]{2,1,0:T(8,128)(2,1)S(1)}, u32[]{:S(2)}, u32[]{:S(2)}) async-start(bf16[4,64,512]{2,1,0:T(8,128)(2,1)} %shard_map.50), calls=%async_computation.3 | async-start | bytes 524288 | tf_op jit(solution)/shard_map/all_to_all | solution.py:239
  87.4 19.3 %all-to-all-start.5 = ((bf16[16,32,256]{2,1,0:T(8,128)(2,1)}), bf16[16,32,256]{2,1,0:T(8,128)(2,1)S(1)}, u32[]{:S(2)}, u32[]{:S(2)}) async-start(bf16[16,32,256]{2,1,0:T(8,128)(2,1)} %bitcast.13), calls=%async_computation.5 | async-start | bytes 524288 | tf_op jit(solution)/shard_map/all_to_all | solution.py:245
  91.8 11.5 %collective-permute-start = (bf16[4,2,128,128]{3,2,1,0:T(8,128)(2,1)S(1)}, bf16[4,2,128,128]{3,2,1,0:T(8,128)(2,1)S(1)}, u32[]{:S(2)}, u32[]{:S(2)}) collective-permute-start(bf16[4,2,128,128]{3,2,1,0:T(8,128)(2,1)S(1)} %get-tuple-element.23), channel_id=1, source_target_pairs={{0,32},{32,0},{1,33},{33,1},{2,34},{34,2},{3,35},{35,3},{4,36},{36... | collective-permute-start | bytes 786440 | tf_op jit(solution)/shard_map/ppermute | solution.py:223
  103.3 9.7 %collective-permute-start.1 = (bf16[2,2,2,128,128]{4,3,2,1,0:T(8,128)(2,1)S(1)}, bf16[2,2,2,128,128]{4,3,2,1,0:T(8,128)(2,1)S(1)}, u32[]{:S(2)}, u32[]{:S(2)}) collective-permute-start(bf16[2,2,2,128,128]{4,3,2,1,0:T(8,128)(2,1)S(1)} %get-tuple-element.15), channel_id=1, source_target_pairs={{0,8},{8,0},{1,9},{9,1},{2,10},{10,2},{3,11},{11,3},{4,12},{12,4},... | collective-permute-start | bytes 786440 | tf_op jit(solution)/shard_map/ppermute | solution.py:226
  107.4 16.8 %all-to-all-start.6 = ((bf16[8,64,256]{2,1,0:T(8,128)(2,1)}), bf16[8,64,256]{2,1,0:T(8,128)(2,1)S(1)}, u32[]{:S(2)}, u32[]{:S(2)}) async-start(bf16[8,64,256]{2,1,0:T(8,128)(2,1)} %shard_map.54), calls=%async_computation.6 | async-start | bytes 524288 | tf_op jit(solution)/shard_map/all_to_all | solution.py:252
  113.0 11.2 %collective-permute-start.2 = (bf16[2,2,2,128,128]{4,3,2,1,0:T(8,128)(2,1)S(1)}, bf16[2,2,2,128,128]{4,3,2,1,0:T(8,128)(2,1)S(1)}, u32[]{:S(2)}, u32[]{:S(2)}) collective-permute-start(bf16[2,2,2,128,128]{4,3,2,1,0:T(8,128)(2,1)S(1)} %get-tuple-element.17), channel_id=1, source_target_pairs={{0,16},{16,0},{1,17},{17,1},{2,18},{18,2},{3,19},{19,3},{4,20},{20... | collective-permute-start | bytes 786440 | tf_op jit(solution)/shard_map/ppermute | solution.py:241

commit v4 on v3

--- a/solution.py
+++ b/solution.py
@@ -14,6 +14,7 @@
 LINE = ("y0", "y1", "y2")
 DEPTH = ("zh0", "zh1")
 COLS = ("xl", "zl", "xh")
+CHIPS = ("core", "xh", "xl", "zl")
 SWAP = [(0, 1), (1, 0)]
 
 ANYWHERE = pl.BlockSpec(memory_space=pl.ANY)
@@ -92,7 +93,7 @@
     )(inputs, upstream, eig)
 
 
-def spread_kernel(parts_ref, own_ref, copies_ref):
+def spread_kernel(parts_ref, own_ref, copies_ref, halves_ref):
     total = parts_ref[0].astype(F32)
     for k in range(1, parts_ref.shape[0]):
         total += parts_ref[k].astype(F32)
@@ -100,12 +101,9 @@
     own_ref[...] = own
     for k in range(copies_ref.shape[0]):
         copies_ref[k] = own
-
-
-def again_kernel(own_ref, out_ref):
     for core in range(2):
         for k in range(8):
-            out_ref[core * 8 + k] = own_ref[:, core * 32 : core * 32 + 32]
+            halves_ref[core * 8 + k] = own[:, core * 32 : core * 32 + 32]
 
 
 def gram_kernel(b_ref, a_ref, other_ref, out_ref):
@@ -207,14 +205,21 @@
     cube = jnp.transpose(eigvals.reshape(2, 2, 8, 2, 64), (0, 3, 1, 2, 4)).reshape(8, 8, 64)
     lam_a = lax.dynamic_index_in_dim(cube, r * 2 + xl, 0, keepdims=False)
     lam_own = lax.dynamic_index_in_dim(lam_a, y, 0, keepdims=False).reshape(64, 1)
-    by_core = lax.dynamic_index_in_dim(lam_b.reshape(4, 2, 2, 32), core, 2, keepdims=False)
+    by_place = jnp.transpose(lam_b.reshape(2, 2, 2, 64), (2, 0, 1, 3)).reshape(4, 2, 2, 32)
+    by_core = lax.dynamic_index_in_dim(by_place, core, 2, keepdims=False)
     lam_rows = lax.dynamic_index_in_dim(by_core, share, 0, keepdims=False).reshape(64, 1)
     lam_cols = jnp.transpose(lam_a.reshape(2, 2, 2, 64), (2, 1, 0, 3)).reshape(1, 512)
 
     parts = project(inputs, upstream, eig)
     got = lax.all_to_all(parts, ROWS, 0, 0, tiled=True)
-    own, copies = call(
-        spread_kernel, (got,), (out(BF16, 2, 64, tokens), out(BF16, 8, 2, 64, tokens))
+    own, copies, pieces = call(
+        spread_kernel,
+        (got,),
+        (
+            out(BF16, 2, 64, tokens),
+            out(BF16, 8, 2, 64, tokens),
+            out(BF16, 16, 2, 32, tokens),
+        ),
     )
     halves = eig.reshape(2, 4, 2, 128, 128)
     right = lax.all_to_all(copies, LINE, 0, 0, tiled=True)
@@ -229,8 +234,7 @@
         (lam_rows, lam_cols, lam_own),
         (out(F32, 64, 1), out(F32, 1, 512), out(F32, 64, 1)),
     )
-    again = call(again_kernel, (own,), out(BF16, 16, 2, 32, tokens))
-    left = lax.all_to_all(again, ("core", *COLS), 0, 0, tiled=True)
+    left = lax.all_to_all(pieces, CHIPS, 0, 0, tiled=True)
     other = lax.ppermute(right, "core", SWAP)
     both = call(
         gram_kernel, (left.reshape(2, 8, 2, 32, tokens), right, other), out(BF16, 4, 64, 512)
@@ -242,7 +246,9 @@
     part = call(weigh_kernel, (shares, s_rows, s_cols), out(BF16, 4, 64, 512))
     mine = lax.all_to_all(part, DEPTH, 0, 0, tiled=True)
     mixed_part = call(mix_kernel, (mine, right, other), out(BF16, 2, 8, 32, tokens))
-    mixed = lax.all_to_all(mixed_part.reshape(16, 32, tokens), ("core", *COLS), 0, 0, tiled=True)
+    mixed = lax.all_to_all(
+        mixed_part.reshape(16, 32, tokens), CHIPS, 0, 0, tiled=True
+    )
     factor = 2.0 / (8 * tokens)
     update = call(
         lambda *refs: update_kernel(factor, *refs),

time: 138 us -> 138 us (level)
  blocking collectives: 38.2 us -> 59.6 us
  waiting for transfers between devices: 46.9 us -> 33.6 us
  starting transfers between devices: 43.2 us -> 35.5 us
    all_to_all x0 -> x1, blocking collectives: none -> 21.2 us  [on_device(): right = lax.all_to_all(copies, LINE, 0, 0, tiled=True)]
    all_to_all x3 -> x2, waiting for transfers between devices: 21.4 us -> 7.95 us  [the longest x1 7.95 us: on_device(): left = lax.all_to_all(pieces, CHIPS, 0, 0, tiled=True)]
    all_to_all x3 -> x2, starting transfers between devices: 15.3 us -> 7.63 us  [the longest x1 4.06 us: on_device(): lax.all_to_all(mixed_part.reshape(16, 32, tokens), CHIPS, 0, 0, tiled=True)]
    pallas_call x10 -> x9, Pallas kernels: 5.19 us -> 4.42 us  [call(): pl.pallas_call(kernel, out_shape=[pltpu.VMEM(s, d) for s, d in shapes_of(...]
  transfers between devices with their start and end apart: 9 -> 8, of which waited for: 6 -> 5; matrix products, arithmetic and copies ran while one was open for 0% -> 0% of each run, Pallas kernels for 1% -> 1%
where the time goes in v4:
time: 138 us; the launch traced here: 137 us
  blocking collectives  59.6 us (43%)
  starting transfers between devices  35.5 us (26%)
  waiting for transfers between devices  33.6 us (24%)
  Pallas kernels  7.08 us (5%)
    all_to_all x1, blocking collectives, on_device(): right = lax.all_to_all(copies, LINE, 0, 0, tiled=True)  21.2 us
    all_to_all x1, blocking collectives, on_device(): got = lax.all_to_all(parts, ROWS, 0, 0, tiled=True)  13.1 us
    all_to_all x1, blocking collectives, on_device(): mine = lax.all_to_all(part, DEPTH, 0, 0, tiled=True)  13 us
    all_to_all x1, blocking collectives, on_device(): blocks = lax.all_to_all(grad_part, LINE, 0, 0, tiled=True)  12.3 us
    all_to_all x1, waiting for transfers between devices, on_device(): shares = lax.all_to_all(both, DEPTH, 0, 0, tiled=True)  10.2 us
    all_to_all x1, starting transfers between devices, on_device(): shares = lax.all_to_all(both, DEPTH, 0, 0, tiled=True)  9.53 us
    all_to_all x1, waiting for transfers between devices, on_device(): left = lax.all_to_all(pieces, CHIPS, 0, 0, tiled=True)  7.95 us
    ppermute x1, waiting for transfers between devices, on_device(): came = lax.ppermute(away, 'zl', SWAP)  7.62 us
  transfers between devices with their start and end apart: 8, of which 5 were waited for; matrix products, arithmetic and copies ran while one was open for 0% of the time, Pallas kernels for 1%

profile of v4, /device:TPU:16, one launch (start us, length us, event | category | flops | bytes accessed | tf_op | source)
XLA Modules:
  0.0 137.3 jit_solution(3286657148740976742)
XLA Ops:
  0.0 2.7 %project.1 = bf16[4,2,64,256]{3,2,1,0:T(8,128)(2,1)S(1)} custom-call(bf16[256,4096]{1,0:T(8,128)(2,1)} %x_ref.1, bf16[256,4096]{1,0:T(8,128)(2,1)} %y_ref.1, bf16[8,2,128,128]{3,2,1,0:T(8,128)(2,1)} %bitcast.23), custom_call_target="tpu_custom_call" | custom-call | tf_op jit(solution)/shard_map/project/pallas_call | solution.py:81
  2.7 13.1 %all_to_all.40.parts_ref = bf16[4,2,64,256]{3,2,1,0:T(8,128)(2,1)S(1)} all-to-all(bf16[4,2,64,256]{3,2,1,0:T(8,128)(2,1)S(1)} %project.1), channel_id=1, replica_groups=mesh['zh1'=2,'zh0'=2,'core'=2,'zl'=2,'xh'=2,'xl'=2,'y2'=2,'y1'=2,'y0'=2]..., dimensions={0} | all-to-all | bytes 524288 | tf_op jit(solution)/shard_map/all_to_all | solution.py:214
  15.8 0.9 shard_map.48
  16.7 21.2 %all_to_all.41.a_ref = bf16[8,2,64,256]{3,2,1,0:T(8,128)(2,1)S(1)} all-to-all(bf16[8,2,64,256]{3,2,1,0:T(8,128)(2,1)S(1)} %get-tuple-element.20), channel_id=1, replica_groups=mesh['zh1'=2,'zh0'=2,'core'=2,'zl'=2,'xh'=2,'xl'=2,'y2'=2,'y1'=2,'y0'=2]..., dimensions={0} | all-to-all | bytes 1048576 | tf_op jit(solution)/shard_map/all_to_all | solution.py:225
  37.9 3.6 %all-to-all-start.1 = ((bf16[16,2,32,256]{3,2,1,0:T(8,128)(2,1)}), bf16[16,2,32,256]{3,2,1,0:T(8,128)(2,1)S(1)}, u32[]{:S(2)}, u32[]{:S(2)}) async-start(bf16[16,2,32,256]{3,2,1,0:T(8,128)(2,1)} %get-tuple-element.19), calls=%async_computation.1 | async-start | bytes 1048576 | tf_op jit(solution)/shard_map/all_to_all | solution.py:237
  41.5 2.2 %collective-permute-start.3 = (bf16[8,2,64,256]{3,2,1,0:T(8,128)(2,1)S(1)}, bf16[8,2,64,256]{3,2,1,0:T(8,128)(2,1)S(1)}, u32[]{:S(2)}, u32[]{:S(2)}) collective-permute-start(bf16[8,2,64,256]{3,2,1,0:T(8,128)(2,1)S(1)} %all_to_all.41.a_ref), channel_id=1, source_target_pairs={{0,64},{64,0},{1,65},{65,1},{2,66},{66,2},{3,67},{67,3},{4,68},{68... | collective-permute-start | bytes 1572872 | tf_op jit(solution)/shard_map/ppermute | solution.py:238
  43.7 7.9 %all-to-all-done.1 = bf16[16,2,32,256]{3,2,1,0:T(8,128)(2,1)S(1)} async-done(((bf16[16,2,32,256]{3,2,1,0:T(8,128)(2,1)}), bf16[16,2,32,256]{3,2,1,0:T(8,128)(2,1)S(1)}, u32[]{:S(2)}, u32[]{:S(2)}) %all-to-all-start.1) | async-done | bytes 524320 | tf_op jit(solution)/shard_map/all_to_all | solution.py:237
  51.6 1.2 shard_map.49
  52.8 9.5 %all-to-all-start.3 = ((bf16[4,64,512]{2,1,0:T(8,128)(2,1)}), bf16[4,64,512]{2,1,0:T(8,128)(2,1)S(1)}, u32[]{:S(2)}, u32[]{:S(2)}) async-start(bf16[4,64,512]{2,1,0:T(8,128)(2,1)} %shard_map.49), calls=%async_computation.3 | async-start | bytes 524288 | tf_op jit(solution)/shard_map/all_to_all | solution.py:243
  63.0 10.2 %all-to-all-done.3.parts_ref = bf16[4,64,512]{2,1,0:T(8,128)(2,1)S(1)} async-done(((bf16[4,64,512]{2,1,0:T(8,128)(2,1)}), bf16[4,64,512]{2,1,0:T(8,128)(2,1)S(1)}, u32[]{:S(2)}, u32[]{:S(2)}) %all-to-all-start.3) | async-done | bytes 262176 | tf_op jit(solution)/shard_map/all_to_all | solution.py:243
  73.3 13.0 %all_to_all.42.half_ref = bf16[4,64,512]{2,1,0:T(8,128)(2,1)S(1)} all-to-all(bf16[4,64,512]{2,1,0:T(8,128)(2,1)S(1)} %shard_map.51), channel_id=1, replica_groups=mesh['zh1'=2,'zh0'=2,'core'=2,'zl'=2,'xh'=2,'xl'=2,'y2'=2,'y1'=2,'y0'=2]..., dimensions={0} | all-to-all | bytes 524288 | tf_op jit(solution)/shard_map/all_to_all | solution.py:247
  86.3 1.0 shard_map.52
  87.3 4.1 %all-to-all-start.5 = ((bf16[16,32,256]{2,1,0:T(8,128)(2,1)}), bf16[16,32,256]{2,1,0:T(8,128)(2,1)S(1)}, u32[]{:S(2)}, u32[]{:S(2)}) async-start(bf16[16,32,256]{2,1,0:T(8,128)(2,1)} %bitcast.14), calls=%async_computation.5 | async-start | bytes 524288 | tf_op jit(solution)/shard_map/all_to_all | solution.py:249
  91.5 3.8 %collective-permute-start = (bf16[4,2,128,128]{3,2,1,0:T(8,128)(2,1)S(1)}, bf16[4,2,128,128]{3,2,1,0:T(8,128)(2,1)S(1)}, u32[]{:S(2)}, u32[]{:S(2)}) collective-permute-start(bf16[4,2,128,128]{3,2,1,0:T(8,128)(2,1)S(1)} %get-tuple-element.25), channel_id=1, source_target_pairs={{0,32},{32,0},{1,33},{33,1},{2,34},{34,2},{3,35},{35,3},{4,36},{36... | collective-permute-start | bytes 786440 | tf_op jit(solution)/shard_map/ppermute | solution.py:228
  95.3 7.6 %collective-permute-done.came_ref = bf16[4,2,128,128]{3,2,1,0:T(8,128)(2,1)S(1)} collective-permute-done((bf16[4,2,128,128]{3,2,1,0:T(8,128)(2,1)S(1)}, bf16[4,2,128,128]{3,2,1,0:T(8,128)(2,1)S(1)}, u32[]{:S(2)}, u32[]{:S(2)}) %collective-permute-start) | collective-permute-done | bytes 262176 | tf_op jit(solution)/shard_map/ppermute | solution.py:228
  103.0 3.4 %collective-permute-start.1 = (bf16[2,2,2,128,128]{4,3,2,1,0:T(8,128)(2,1)S(1)}, bf16[2,2,2,128,128]{4,3,2,1,0:T(8,128)(2,1)S(1)}, u32[]{:S(2)}, u32[]{:S(2)}) collective-permute-start(bf16[2,2,2,128,128]{4,3,2,1,0:T(8,128)(2,1)S(1)} %get-tuple-element.16), channel_id=1, source_target_pairs={{0,8},{8,0},{1,9},{9,1},{2,10},{10,2},{3,11},{11,3},{4,12},{12,4},... | collective-permute-start | bytes 786440 | tf_op jit(solution)/shard_map/ppermute | solution.py:231
  106.4 0.8 shard_map.53
  107.2 4.1 %all-to-all-start.6 = ((bf16[8,64,256]{2,1,0:T(8,128)(2,1)}), bf16[8,64,256]{2,1,0:T(8,128)(2,1)S(1)}, u32[]{:S(2)}, u32[]{:S(2)}) async-start(bf16[8,64,256]{2,1,0:T(8,128)(2,1)} %shard_map.53), calls=%async_computation.6 | async-start | bytes 524288 | tf_op jit(solution)/shard_map/all_to_all | solution.py:258
  111.2 1.5 %collective-permute-done.1.came_ref = bf16[2,2,2,128,128]{4,3,2,1,0:T(8,128)(2,1)S(1)} collective-permute-done((bf16[2,2,2,128,128]{4,3,2,1,0:T(8,128)(2,1)S(1)}, bf16[2,2,2,128,128]{4,3,2,1,0:T(8,128)(2,1)S(1)}, u32[]{:S(2)}, u32[]{:S(2)}) %collective-permute-start.1) | collective-permute-done | bytes 262176 | tf_op jit(solution)/shard_map/ppermute | solution.py:231
  112.7 4.8 %collective-permute-start.2 = (bf16[2,2,2,128,128]{4,3,2,1,0:T(8,128)(2,1)S(1)}, bf16[2,2,2,128,128]{4,3,2,1,0:T(8,128)(2,1)S(1)}, u32[]{:S(2)}, u32[]{:S(2)}) collective-permute-start(bf16[2,2,2,128,128]{4,3,2,1,0:T(8,128)(2,1)S(1)} %get-tuple-element.18), channel_id=1, source_target_pairs={{0,16},{16,0},{1,17},{17,1},{2,18},{18,2},{3,19},{19,3},{4,20},{20... | collective-permute-start | bytes 786440 | tf_op jit(solution)/shard_map/ppermute | solution.py:245
  117.6 6.4 %collective-permute-done.2.came_ref = bf16[2,2,2,128,128]{4,3,2,1,0:T(8,128)(2,1)S(1)} collective-permute-done((bf16[2,2,2,128,128]{4,3,2,1,0:T(8,128)(2,1)S(1)}, bf16[2,2,2,128,128]{4,3,2,1,0:T(8,128)(2,1)S(1)}, u32[]{:S(2)}, u32[]{:S(2)}) %collective-permute-start.2) | collective-permute-done | bytes 262176 | tf_op jit(solution)/shard_map/ppermute | solution.py:245
  124.0 0.3 shard_map.54
  124.3 12.3 %all_to_all.43 = bf16[8,64,256]{2,1,0:T(8,128)(2,1)S(1)} all-to-all(bf16[8,64,256]{2,1,0:T(8,128)(2,1)S(1)} %shard_map.54), channel_id=1, replica_groups=mesh['zh1'=2,'zh0'=2,'core'=2,'zl'=2,'xh'=2,'xl'=2,'y2'=2,'y1'=2,'y0'=2]..., dimensions={0} | all-to-all | bytes 524288 | tf_op jit(solution)/shard_map/all_to_all | solution.py:265
  136.6 0.7 reduce_sum.12
  (26 shorter events, 0.9 us)
Async XLA Ops:
  16.7 45.6 %copy-start.1 = (f32[4096]{0:T(1024)S(1)}, f32[4096]{0:T(1024)}, u32[]{:S(2)}) copy-start(f32[4096]{0:T(1024)} %param.7) | copy-start | bytes 49156
  37.9 13.8 %all-to-all-start.1 = ((bf16[16,2,32,256]{3,2,1,0:T(8,128)(2,1)}), bf16[16,2,32,256]{3,2,1,0:T(8,128)(2,1)S(1)}, u32[]{:S(2)}, u32[]{:S(2)}) async-start(bf16[16,2,32,256]{3,2,1,0:T(8,128)(2,1)} %get-tuple-element.19), calls=%async_computation.1 | async-start | bytes 1048576 | tf_op jit(solution)/shard_map/all_to_all | solution.py:237
  41.5 10.2 %collective-permute-start.3 = (bf16[8,2,64,256]{3,2,1,0:T(8,128)(2,1)S(1)}, bf16[8,2,64,256]{3,2,1,0:T(8,128)(2,1)S(1)}, u32[]{:S(2)}, u32[]{:S(2)}) collective-permute-start(bf16[8,2,64,256]{3,2,1,0:T(8,128)(2,1)S(1)} %all_to_all.41.a_ref), channel_id=1, source_target_pairs={{0,64},{64,0},{1,65},{65,1},{2,66},{66,2},{3,67},{67,3},{4,68},{68... | collective-permute-start | bytes 1572872 | tf_op jit(solution)/shard_map/ppermute | solution.py:238
  52.8 38.6 %copy-start = (bf16[1,8,2,128,128]{4,3,2,1,0:T(8,128)(2,1)S(1)}, bf16[1,8,2,128,128]{4,3,2,1,0:T(8,128)(2,1)}, u32[]{:S(2)}) copy-start(bf16[1,8,2,128,128]{4,3,2,1,0:T(8,128)(2,1)} %param.6) | copy-start | bytes 1572868
  52.8 20.4 %all-to-all-start.3 = ((bf16[4,64,512]{2,1,0:T(8,128)(2,1)}), bf16[4,64,512]{2,1,0:T(8,128)(2,1)S(1)}, u32[]{:S(2)}, u32[]{:S(2)}) async-start(bf16[4,64,512]{2,1,0:T(8,128)(2,1)} %shard_map.49), calls=%async_computation.3 | async-start | bytes 524288 | tf_op jit(solution)/shard_map/all_to_all | solution.py:243
  87.3 19.0 %all-to-all-start.5 = ((bf16[16,32,256]{2,1,0:T(8,128)(2,1)}), bf16[16,32,256]{2,1,0:T(8,128)(2,1)S(1)}, u32[]{:S(2)}, u32[]{:S(2)}) async-start(bf16[16,32,256]{2,1,0:T(8,128)(2,1)} %bitcast.14), calls=%async_computation.5 | async-start | bytes 524288 | tf_op jit(solution)/shard_map/all_to_all | solution.py:249
  91.5 11.5 %collective-permute-start = (bf16[4,2,128,128]{3,2,1,0:T(8,128)(2,1)S(1)}, bf16[4,2,128,128]{3,2,1,0:T(8,128)(2,1)S(1)}, u32[]{:S(2)}, u32[]{:S(2)}) collective-permute-start(bf16[4,2,128,128]{3,2,1,0:T(8,128)(2,1)S(1)} %get-tuple-element.25), channel_id=1, source_target_pairs={{0,32},{32,0},{1,33},{33,1},{2,34},{34,2},{3,35},{35,3},{4,36},{36... | collective-permute-start | bytes 786440 | tf_op jit(solution)/shard_map/ppermute | solution.py:228
  103.0 9.7 %collective-permute-start.1 = (bf16[2,2,2,128,128]{4,3,2,1,0:T(8,128)(2,1)S(1)}, bf16[2,2,2,128,128]{4,3,2,1,0:T(8,128)(2,1)S(1)}, u32[]{:S(2)}, u32[]{:S(2)}) collective-permute-start(bf16[2,2,2,128,128]{4,3,2,1,0:T(8,128)(2,1)S(1)} %get-tuple-element.16), channel_id=1, source_target_pairs={{0,8},{8,0},{1,9},{9,1},{2,10},{10,2},{3,11},{11,3},{4,12},{12,4},... | collective-permute-start | bytes 786440 | tf_op jit(solution)/shard_map/ppermute | solution.py:231
  107.2 16.8 %all-to-all-start.6 = ((bf16[8,64,256]{2,1,0:T(8,128)(2,1)}), bf16[8,64,256]{2,1,0:T(8,128)(2,1)S(1)}, u32[]{:S(2)}, u32[]{:S(2)}) async-start(bf16[8,64,256]{2,1,0:T(8,128)(2,1)} %shard_map.53), calls=%async_computation.6 | async-start | bytes 524288 | tf_op jit(solution)/shard_map/all_to_all | solution.py:258
  112.7 11.2 %collective-permute-start.2 = (bf16[2,2,2,128,128]{4,3,2,1,0:T(8,128)(2,1)S(1)}, bf16[2,2,2,128,128]{4,3,2,1,0:T(8,128)(2,1)S(1)}, u32[]{:S(2)}, u32[]{:S(2)}) collective-permute-start(bf16[2,2,2,128,128]{4,3,2,1,0:T(8,128)(2,1)S(1)} %get-tuple-element.18), channel_id=1, source_target_pairs={{0,16},{16,0},{1,17},{17,1},{2,18},{18,2},{3,19},{19,3},{4,20},{20... | collective-permute-start | bytes 786440 | tf_op jit(solution)/shard_map/ppermute | solution.py:245

commit v5 on v3

--- a/solution.py
+++ b/solution.py
@@ -14,6 +14,7 @@
 LINE = ("y0", "y1", "y2")
 DEPTH = ("zh0", "zh1")
 COLS = ("xl", "zl", "xh")
+CHIPS = ("core", "xh", "xl", "zl")
 SWAP = [(0, 1), (1, 0)]
 
 ANYWHERE = pl.BlockSpec(memory_space=pl.ANY)
@@ -67,7 +68,7 @@
         for la in range(steps):
             copy(s, la).wait()
         part = jnp.dot(xs[s], basis, preferred_element_type=F32)
-        turned = part.T.astype(BF16)
+        turned = part.astype(BF16).T
         turned = turned.reshape(out_ref.shape[0], *out_ref.shape[2:])
         for zl in range(2):
             for xh in range(2):
@@ -207,7 +208,8 @@
     cube = jnp.transpose(eigvals.reshape(2, 2, 8, 2, 64), (0, 3, 1, 2, 4)).reshape(8, 8, 64)
     lam_a = lax.dynamic_index_in_dim(cube, r * 2 + xl, 0, keepdims=False)
     lam_own = lax.dynamic_index_in_dim(lam_a, y, 0, keepdims=False).reshape(64, 1)
-    by_core = lax.dynamic_index_in_dim(lam_b.reshape(4, 2, 2, 32), core, 2, keepdims=False)
+    by_place = jnp.transpose(lam_b.reshape(2, 2, 2, 64), (2, 0, 1, 3)).reshape(4, 2, 2, 32)
+    by_core = lax.dynamic_index_in_dim(by_place, core, 2, keepdims=False)
     lam_rows = lax.dynamic_index_in_dim(by_core, share, 0, keepdims=False).reshape(64, 1)
     lam_cols = jnp.transpose(lam_a.reshape(2, 2, 2, 64), (2, 1, 0, 3)).reshape(1, 512)
 
@@ -230,7 +232,7 @@
         (out(F32, 64, 1), out(F32, 1, 512), out(F32, 64, 1)),
     )
     again = call(again_kernel, (own,), out(BF16, 16, 2, 32, tokens))
-    left = lax.all_to_all(again, ("core", *COLS), 0, 0, tiled=True)
+    left = lax.all_to_all(again, CHIPS, 0, 0, tiled=True)
     other = lax.ppermute(right, "core", SWAP)
     both = call(
         gram_kernel, (left.reshape(2, 8, 2, 32, tokens), right, other), out(BF16, 4, 64, 512)
@@ -242,7 +244,9 @@
     part = call(weigh_kernel, (shares, s_rows, s_cols), out(BF16, 4, 64, 512))
     mine = lax.all_to_all(part, DEPTH, 0, 0, tiled=True)
     mixed_part = call(mix_kernel, (mine, right, other), out(BF16, 2, 8, 32, tokens))
-    mixed = lax.all_to_all(mixed_part.reshape(16, 32, tokens), ("core", *COLS), 0, 0, tiled=True)
+    mixed = lax.all_to_all(
+        mixed_part.reshape(16, 32, tokens), CHIPS, 0, 0, tiled=True
+    )
     factor = 2.0 / (8 * tokens)
     update = call(
         lambda *refs: update_kernel(factor, *refs),

time: 138 us -> 138 us (level)
  no operation moved by 1% of the time
where the time goes in v5:
time: 138 us; the launch traced here: 137 us
  waiting for transfers between devices  46.6 us (34%)
  starting transfers between devices  42.9 us (31%)
  blocking collectives  38.4 us (28%)
  Pallas kernels  7.82 us (6%)
    all_to_all x1, blocking collectives, on_device(): got = lax.all_to_all(parts, ROWS, 0, 0, tiled=True)  13.1 us
    all_to_all x1, blocking collectives, on_device(): mine = lax.all_to_all(part, DEPTH, 0, 0, tiled=True)  13 us
    all_to_all x1, waiting for transfers between devices, on_device(): right = lax.all_to_all(copies, LINE, 0, 0, tiled=True)  13 us
    all_to_all x1, blocking collectives, on_device(): blocks = lax.all_to_all(grad_part, LINE, 0, 0, tiled=True)  12.3 us
    all_to_all x1, waiting for transfers between devices, on_device(): shares = lax.all_to_all(both, DEPTH, 0, 0, tiled=True)  10.2 us
    all_to_all x1, starting transfers between devices, on_device(): shares = lax.all_to_all(both, DEPTH, 0, 0, tiled=True)  9.53 us
    all_to_all x1, waiting for transfers between devices, on_device(): left = lax.all_to_all(again, CHIPS, 0, 0, tiled=True)  7.95 us
    ppermute x1, waiting for transfers between devices, on_device(): came = lax.ppermute(away, 'zl', SWAP)  7.62 us
  transfers between devices with their start and end apart: 9, of which 6 were waited for; matrix products, arithmetic and copies ran while one was open for 0% of the time, Pallas kernels for 1%

profile of v5, /device:TPU:16, one launch (start us, length us, event | category | flops | bytes accessed | tf_op | source)
XLA Modules:
  0.0 137.3 jit_solution(16415470202262215639)
XLA Ops:
  0.0 2.6 %project.1 = bf16[4,2,64,256]{3,2,1,0:T(8,128)(2,1)S(1)} custom-call(bf16[256,4096]{1,0:T(8,128)(2,1)} %x_ref.1, bf16[256,4096]{1,0:T(8,128)(2,1)} %y_ref.1, bf16[8,2,128,128]{3,2,1,0:T(8,128)(2,1)} %bitcast.23), custom_call_target="tpu_custom_call" | custom-call | tf_op jit(solution)/shard_map/project/pallas_call | solution.py:81
  2.6 13.1 %all_to_all.40.parts_ref = bf16[4,2,64,256]{3,2,1,0:T(8,128)(2,1)S(1)} all-to-all(bf16[4,2,64,256]{3,2,1,0:T(8,128)(2,1)S(1)} %project.1), channel_id=1, replica_groups=mesh['zh1'=2,'zh0'=2,'core'=2,'zl'=2,'xh'=2,'xl'=2,'y2'=2,'y1'=2,'y0'=2]..., dimensions={0} | all-to-all | bytes 524288 | tf_op jit(solution)/shard_map/all_to_all | solution.py:217
  15.8 0.8 shard_map.48
  16.6 7.4 %all-to-all-start.2 = ((bf16[8,2,64,256]{3,2,1,0:T(8,128)(2,1)}), bf16[8,2,64,256]{3,2,1,0:T(8,128)(2,1)S(1)}, u32[]{:S(2)}, u32[]{:S(2)}) async-start(bf16[8,2,64,256]{3,2,1,0:T(8,128)(2,1)} %get-tuple-element.19), calls=%async_computation.2 | async-start | bytes 1048576 | tf_op jit(solution)/shard_map/all_to_all | solution.py:222
  24.0 0.8 shard_map.49
  24.9 13.0 %all-to-all-done.2.a_ref = bf16[8,2,64,256]{3,2,1,0:T(8,128)(2,1)S(1)} async-done(((bf16[8,2,64,256]{3,2,1,0:T(8,128)(2,1)}), bf16[8,2,64,256]{3,2,1,0:T(8,128)(2,1)S(1)}, u32[]{:S(2)}, u32[]{:S(2)}) %all-to-all-start.2) | async-done | bytes 524320 | tf_op jit(solution)/shard_map/all_to_all | solution.py:222
  37.9 3.6 %all-to-all-start.1 = ((bf16[16,2,32,256]{3,2,1,0:T(8,128)(2,1)}), bf16[16,2,32,256]{3,2,1,0:T(8,128)(2,1)S(1)}, u32[]{:S(2)}, u32[]{:S(2)}) async-start(bf16[16,2,32,256]{3,2,1,0:T(8,128)(2,1)} %shard_map.49), calls=%async_computation.1 | async-start | bytes 1048576 | tf_op jit(solution)/shard_map/all_to_all | solution.py:235
  41.4 2.2 %collective-permute-start.3 = (bf16[8,2,64,256]{3,2,1,0:T(8,128)(2,1)S(1)}, bf16[8,2,64,256]{3,2,1,0:T(8,128)(2,1)S(1)}, u32[]{:S(2)}, u32[]{:S(2)}) collective-permute-start(bf16[8,2,64,256]{3,2,1,0:T(8,128)(2,1)S(1)} %all-to-all-done.2.a_ref), channel_id=1, source_target_pairs={{0,64},{64,0},{1,65},{65,1},{2,66},{66,2},{3,67},{67,3},{4,68},{68... | collective-permute-start | bytes 1572872 | tf_op jit(solution)/shard_map/ppermute | solution.py:236
  43.7 7.9 %all-to-all-done.1 = bf16[16,2,32,256]{3,2,1,0:T(8,128)(2,1)S(1)} async-done(((bf16[16,2,32,256]{3,2,1,0:T(8,128)(2,1)}), bf16[16,2,32,256]{3,2,1,0:T(8,128)(2,1)S(1)}, u32[]{:S(2)}, u32[]{:S(2)}) %all-to-all-start.1) | async-done | bytes 524320 | tf_op jit(solution)/shard_map/all_to_all | solution.py:235
  51.6 1.2 shard_map.50
  52.8 9.5 %all-to-all-start.3 = ((bf16[4,64,512]{2,1,0:T(8,128)(2,1)}), bf16[4,64,512]{2,1,0:T(8,128)(2,1)S(1)}, u32[]{:S(2)}, u32[]{:S(2)}) async-start(bf16[4,64,512]{2,1,0:T(8,128)(2,1)} %shard_map.50), calls=%async_computation.3 | async-start | bytes 524288 | tf_op jit(solution)/shard_map/all_to_all | solution.py:241
  63.0 10.2 %all-to-all-done.3.parts_ref = bf16[4,64,512]{2,1,0:T(8,128)(2,1)S(1)} async-done(((bf16[4,64,512]{2,1,0:T(8,128)(2,1)}), bf16[4,64,512]{2,1,0:T(8,128)(2,1)S(1)}, u32[]{:S(2)}, u32[]{:S(2)}) %all-to-all-start.3) | async-done | bytes 262176 | tf_op jit(solution)/shard_map/all_to_all | solution.py:241
  73.3 13.0 %all_to_all.41.half_ref = bf16[4,64,512]{2,1,0:T(8,128)(2,1)S(1)} all-to-all(bf16[4,64,512]{2,1,0:T(8,128)(2,1)S(1)} %shard_map.52), channel_id=1, replica_groups=mesh['zh1'=2,'zh0'=2,'core'=2,'zl'=2,'xh'=2,'xl'=2,'y2'=2,'y1'=2,'y0'=2]..., dimensions={0} | all-to-all | bytes 524288 | tf_op jit(solution)/shard_map/all_to_all | solution.py:245
  86.3 1.0 shard_map.53
  87.3 4.1 %all-to-all-start.5 = ((bf16[16,32,256]{2,1,0:T(8,128)(2,1)}), bf16[16,32,256]{2,1,0:T(8,128)(2,1)S(1)}, u32[]{:S(2)}, u32[]{:S(2)}) async-start(bf16[16,32,256]{2,1,0:T(8,128)(2,1)} %bitcast.14), calls=%async_computation.5 | async-start | bytes 524288 | tf_op jit(solution)/shard_map/all_to_all | solution.py:247
  91.5 3.8 %collective-permute-start = (bf16[4,2,128,128]{3,2,1,0:T(8,128)(2,1)S(1)}, bf16[4,2,128,128]{3,2,1,0:T(8,128)(2,1)S(1)}, u32[]{:S(2)}, u32[]{:S(2)}) collective-permute-start(bf16[4,2,128,128]{3,2,1,0:T(8,128)(2,1)S(1)} %get-tuple-element.23), channel_id=1, source_target_pairs={{0,32},{32,0},{1,33},{33,1},{2,34},{34,2},{3,35},{35,3},{4,36},{36... | collective-permute-start | bytes 786440 | tf_op jit(solution)/shard_map/ppermute | solution.py:225
  95.3 7.6 %collective-permute-done.came_ref = bf16[4,2,128,128]{3,2,1,0:T(8,128)(2,1)S(1)} collective-permute-done((bf16[4,2,128,128]{3,2,1,0:T(8,128)(2,1)S(1)}, bf16[4,2,128,128]{3,2,1,0:T(8,128)(2,1)S(1)}, u32[]{:S(2)}, u32[]{:S(2)}) %collective-permute-start) | collective-permute-done | bytes 262176 | tf_op jit(solution)/shard_map/ppermute | solution.py:225
  103.0 3.4 %collective-permute-start.1 = (bf16[2,2,2,128,128]{4,3,2,1,0:T(8,128)(2,1)S(1)}, bf16[2,2,2,128,128]{4,3,2,1,0:T(8,128)(2,1)S(1)}, u32[]{:S(2)}, u32[]{:S(2)}) collective-permute-start(bf16[2,2,2,128,128]{4,3,2,1,0:T(8,128)(2,1)S(1)} %get-tuple-element.15), channel_id=1, source_target_pairs={{0,8},{8,0},{1,9},{9,1},{2,10},{10,2},{3,11},{11,3},{4,12},{12,4},... | collective-permute-start | bytes 786440 | tf_op jit(solution)/shard_map/ppermute | solution.py:228
  106.3 0.8 shard_map.54
  107.1 4.1 %all-to-all-start.6 = ((bf16[8,64,256]{2,1,0:T(8,128)(2,1)}), bf16[8,64,256]{2,1,0:T(8,128)(2,1)S(1)}, u32[]{:S(2)}, u32[]{:S(2)}) async-start(bf16[8,64,256]{2,1,0:T(8,128)(2,1)} %shard_map.54), calls=%async_computation.6 | async-start | bytes 524288 | tf_op jit(solution)/shard_map/all_to_all | solution.py:256
  111.2 1.5 %collective-permute-done.1.came_ref = bf16[2,2,2,128,128]{4,3,2,1,0:T(8,128)(2,1)S(1)} collective-permute-done((bf16[2,2,2,128,128]{4,3,2,1,0:T(8,128)(2,1)S(1)}, bf16[2,2,2,128,128]{4,3,2,1,0:T(8,128)(2,1)S(1)}, u32[]{:S(2)}, u32[]{:S(2)}) %collective-permute-start.1) | collective-permute-done | bytes 262176 | tf_op jit(solution)/shard_map/ppermute | solution.py:228
  112.7 4.8 %collective-permute-start.2 = (bf16[2,2,2,128,128]{4,3,2,1,0:T(8,128)(2,1)S(1)}, bf16[2,2,2,128,128]{4,3,2,1,0:T(8,128)(2,1)S(1)}, u32[]{:S(2)}, u32[]{:S(2)}) collective-permute-start(bf16[2,2,2,128,128]{4,3,2,1,0:T(8,128)(2,1)S(1)} %get-tuple-element.17), channel_id=1, source_target_pairs={{0,16},{16,0},{1,17},{17,1},{2,18},{18,2},{3,19},{19,3},{4,20},{20... | collective-permute-start | bytes 786440 | tf_op jit(solution)/shard_map/ppermute | solution.py:243
  117.6 6.4 %collective-permute-done.2.came_ref = bf16[2,2,2,128,128]{4,3,2,1,0:T(8,128)(2,1)S(1)} collective-permute-done((bf16[2,2,2,128,128]{4,3,2,1,0:T(8,128)(2,1)S(1)}, bf16[2,2,2,128,128]{4,3,2,1,0:T(8,128)(2,1)S(1)}, u32[]{:S(2)}, u32[]{:S(2)}) %collective-permute-start.2) | collective-permute-done | bytes 262176 | tf_op jit(solution)/shard_map/ppermute | solution.py:243
  124.3 12.3 %all_to_all.42 = bf16[8,64,256]{2,1,0:T(8,128)(2,1)S(1)} all-to-all(bf16[8,64,256]{2,1,0:T(8,128)(2,1)S(1)} %shard_map.55), channel_id=1, replica_groups=mesh['zh1'=2,'zh0'=2,'core'=2,'zl'=2,'xh'=2,'xl'=2,'y2'=2,'y1'=2,'y0'=2]..., dimensions={0} | all-to-all | bytes 524288 | tf_op jit(solution)/shard_map/all_to_all | solution.py:263
  (28 shorter events, 1.9 us)
Async XLA Ops:
  16.6 21.2 %all-to-all-start.2 = ((bf16[8,2,64,256]{3,2,1,0:T(8,128)(2,1)}), bf16[8,2,64,256]{3,2,1,0:T(8,128)(2,1)S(1)}, u32[]{:S(2)}, u32[]{:S(2)}) async-start(bf16[8,2,64,256]{3,2,1,0:T(8,128)(2,1)} %get-tuple-element.19), calls=%async_computation.2 | async-start | bytes 1048576 | tf_op jit(solution)/shard_map/all_to_all | solution.py:222
  24.0 38.3 %copy-start.1 = (f32[4096]{0:T(1024)S(1)}, f32[4096]{0:T(1024)}, u32[]{:S(2)}) copy-start(f32[4096]{0:T(1024)} %param.7) | copy-start | bytes 49156
  37.9 13.8 %all-to-all-start.1 = ((bf16[16,2,32,256]{3,2,1,0:T(8,128)(2,1)}), bf16[16,2,32,256]{3,2,1,0:T(8,128)(2,1)S(1)}, u32[]{:S(2)}, u32[]{:S(2)}) async-start(bf16[16,2,32,256]{3,2,1,0:T(8,128)(2,1)} %shard_map.49), calls=%async_computation.1 | async-start | bytes 1048576 | tf_op jit(solution)/shard_map/all_to_all | solution.py:235
  41.4 10.2 %collective-permute-start.3 = (bf16[8,2,64,256]{3,2,1,0:T(8,128)(2,1)S(1)}, bf16[8,2,64,256]{3,2,1,0:T(8,128)(2,1)S(1)}, u32[]{:S(2)}, u32[]{:S(2)}) collective-permute-start(bf16[8,2,64,256]{3,2,1,0:T(8,128)(2,1)S(1)} %all-to-all-done.2.a_ref), channel_id=1, source_target_pairs={{0,64},{64,0},{1,65},{65,1},{2,66},{66,2},{3,67},{67,3},{4,68},{68... | collective-permute-start | bytes 1572872 | tf_op jit(solution)/shard_map/ppermute | solution.py:236
  52.8 38.6 %copy-start = (bf16[1,8,2,128,128]{4,3,2,1,0:T(8,128)(2,1)S(1)}, bf16[1,8,2,128,128]{4,3,2,1,0:T(8,128)(2,1)}, u32[]{:S(2)}) copy-start(bf16[1,8,2,128,128]{4,3,2,1,0:T(8,128)(2,1)} %param.6) | copy-start | bytes 1572868
  52.8 20.4 %all-to-all-start.3 = ((bf16[4,64,512]{2,1,0:T(8,128)(2,1)}), bf16[4,64,512]{2,1,0:T(8,128)(2,1)S(1)}, u32[]{:S(2)}, u32[]{:S(2)}) async-start(bf16[4,64,512]{2,1,0:T(8,128)(2,1)} %shard_map.50), calls=%async_computation.3 | async-start | bytes 524288 | tf_op jit(solution)/shard_map/all_to_all | solution.py:241
  87.3 19.0 %all-to-all-start.5 = ((bf16[16,32,256]{2,1,0:T(8,128)(2,1)}), bf16[16,32,256]{2,1,0:T(8,128)(2,1)S(1)}, u32[]{:S(2)}, u32[]{:S(2)}) async-start(bf16[16,32,256]{2,1,0:T(8,128)(2,1)} %bitcast.14), calls=%async_computation.5 | async-start | bytes 524288 | tf_op jit(solution)/shard_map/all_to_all | solution.py:247
  91.5 11.5 %collective-permute-start = (bf16[4,2,128,128]{3,2,1,0:T(8,128)(2,1)S(1)}, bf16[4,2,128,128]{3,2,1,0:T(8,128)(2,1)S(1)}, u32[]{:S(2)}, u32[]{:S(2)}) collective-permute-start(bf16[4,2,128,128]{3,2,1,0:T(8,128)(2,1)S(1)} %get-tuple-element.23), channel_id=1, source_target_pairs={{0,32},{32,0},{1,33},{33,1},{2,34},{34,2},{3,35},{35,3},{4,36},{36... | collective-permute-start | bytes 786440 | tf_op jit(solution)/shard_map/ppermute | solution.py:225
  103.0 9.7 %collective-permute-start.1 = (bf16[2,2,2,128,128]{4,3,2,1,0:T(8,128)(2,1)S(1)}, bf16[2,2,2,128,128]{4,3,2,1,0:T(8,128)(2,1)S(1)}, u32[]{:S(2)}, u32[]{:S(2)}) collective-permute-start(bf16[2,2,2,128,128]{4,3,2,1,0:T(8,128)(2,1)S(1)} %get-tuple-element.15), channel_id=1, source_target_pairs={{0,8},{8,0},{1,9},{9,1},{2,10},{10,2},{3,11},{11,3},{4,12},{12,4},... | collective-permute-start | bytes 786440 | tf_op jit(solution)/shard_map/ppermute | solution.py:228
  107.1 16.8 %all-to-all-start.6 = ((bf16[8,64,256]{2,1,0:T(8,128)(2,1)}), bf16[8,64,256]{2,1,0:T(8,128)(2,1)S(1)}, u32[]{:S(2)}, u32[]{:S(2)}) async-start(bf16[8,64,256]{2,1,0:T(8,128)(2,1)} %shard_map.54), calls=%async_computation.6 | async-start | bytes 524288 | tf_op jit(solution)/shard_map/all_to_all | solution.py:256
  112.7 11.2 %collective-permute-start.2 = (bf16[2,2,2,128,128]{4,3,2,1,0:T(8,128)(2,1)S(1)}, bf16[2,2,2,128,128]{4,3,2,1,0:T(8,128)(2,1)S(1)}, u32[]{:S(2)}, u32[]{:S(2)}) collective-permute-start(bf16[2,2,2,128,128]{4,3,2,1,0:T(8,128)(2,1)S(1)} %get-tuple-element.17), channel_id=1, source_target_pairs={{0,16},{16,0},{1,17},{17,1},{2,18},{18,2},{3,19},{19,3},{4,20},{20... | collective-permute-start | bytes 786440 | tf_op jit(solution)/shard_map/ppermute | solution.py:243
